TPU v7x, 32 devices: a whole 2x2x4 slice. The times are simulated.
32 devices in a mesh: rep: 4 (over y, core), row: 4 (over z), col: 2 (over x).
Axes of the slice: x: 2, y: 2, z: 4, core: 2. Of those that a mesh axis runs over, the one named last changes fastest.
Arguments:
- patches: bfloat16 [4096, 588], P(('rep', 'col')), may hold values from -20 to 20
- embed_weight: bfloat16 [588, 6144], P(None, 'row'), may hold values from -1 to 1
- embed_bias: float32 [6144], P('row'), may hold values from -3 to 3
- old_in: bfloat16 [64, 768, 1536], P(('row', 'col')), may hold values from -0.078125 to 0.078125
- old_out: bfloat16 [64, 1536, 768], P(('row', 'col')), may hold values from -0.0546875 to 0.0546875
- restore_id: int32 [1], replicated, may hold values from 0 to 47
- norm_gains: float32 [48, 6144], P(None, 'row'), may hold values from 0.1 to 1.9
- in_biases: float32 [48, 12288], P(None, 'col'), may hold values from -3 to 3
- out_biases: float32 [48, 6144], P(None, 'row'), may hold values from -3 to 3
- final_gain: float32 [6144], P('row'), may hold values from 0.1 to 1.9
- check_weight: bfloat16 [6144, 128], P('row'), may hold values from -0.078125 to 0.078125
Outputs:
- in_weight: bfloat16 [6144, 12288], P('row', 'col')
- out_weight: bfloat16 [12288, 6144], P('col', 'row')
- check_logits: float32 [4096, 128], P(('rep', 'col'))
All inputs are finite; a program needn't handle non-finite values.
Results may differ from a plain program's by a relative error of at most 0.0062.
Values may be sent and summed in bfloat16 or wider, within the bound.
No kernel may reach another device: no remote copies, remote signals or barrier semaphores. Data moves between devices by JAX's collectives and lax.ppermute only.
A program may use at most 192 MiB of HBM per device.

v0:
```python
import jax
import jax.numpy as jnp
from jax import lax
from jax.sharding import PartitionSpec as P

EPSILON = 1e-06


def for_sending(shard):
    return jax.tree.map(lambda a: a.astype(jnp.bfloat16) if a.dtype == jnp.float32 else a, shard)


def partner(value, axis, bit):
    mask = 2**bit
    pairs = [(source, source ^ mask) for source in range(lax.axis_size(axis))]
    return lax.ppermute(value, axis, pairs)


def pick_rows(restore_id, param_table):
    selector = (
        jnp.arange(param_table.shape[0], dtype=jnp.int32)[None, :] == restore_id[:, None]
    ).astype(jnp.float32)
    return jnp.dot(selector, param_table, precision=lax.Precision.HIGHEST)[0]


def norm_rows(values, gain_row):
    feature_count = values.shape[1] * lax.axis_size("row")
    totals = lax.psum((jnp.sum(values, axis=1), jnp.sum(values * values, axis=1)), "row")
    average = totals[0][:, None] / feature_count
    spread = totals[1][:, None] / feature_count - average * average
    return ((values - average) * lax.rsqrt(spread + EPSILON) * gain_row).astype(jnp.bfloat16)


def move_halves(pieces, bit_total, device_index, exchange):
    for bit_number in range(bit_total):
        upper_side = device_index >> bit_number & 1 == 1
        outgoing = tuple(
            (jnp.where(upper_side, lower_part, upper_part) for lower_part, upper_part in pieces)
        )
        incoming = exchange(outgoing, bit_number)
        pieces = tuple(
            (
                (
                    jnp.where(upper_side, arrived, lower_part),
                    jnp.where(upper_side, upper_part, arrived),
                )
                for (lower_part, upper_part), arrived in zip(pieces, incoming)
            )
        )
    return pieces


def on_device(
    patches,
    embed_weight,
    embed_bias,
    old_in,
    old_out,
    restore_id,
    norm_gains,
    in_biases,
    out_biases,
    final_gain,
    check_weight,
):
    tiles_here, tile_rows, tile_cols = old_in.shape
    local_cols = tiles_here * tile_cols
    half_cols = local_cols // 2
    in_local = jnp.transpose(old_in, (1, 0, 2)).reshape(tile_rows, local_cols)
    out_local = old_out.reshape(local_cols, tile_rows)
    col_index = lax.axis_index("col")
    col_count = lax.axis_size("col")
    col_bits = col_count.bit_length() - 1
    pieces = (
        (in_local[:, :half_cols], in_local[:, half_cols:]),
        (out_local[:half_cols], out_local[half_cols:]),
    )
    pieces = move_halves(
        pieces,
        col_bits,
        col_index,
        lambda send_parts, bit_number: jax.tree.map(
            lambda part, own: part.astype(own.dtype),
            partner(for_sending(send_parts), "col", bit_number),
            send_parts,
        ),
    )
    in_pair, out_pair = pieces
    in_weight = jnp.concatenate(in_pair, axis=0)
    out_weight = jnp.concatenate(out_pair, axis=1)
    layer_gain = pick_rows(restore_id, norm_gains)
    in_bias = pick_rows(restore_id, in_biases)
    out_bias = pick_rows(restore_id, out_biases)
    embedded = jnp.dot(patches, embed_weight, preferred_element_type=jnp.float32) + embed_bias
    normed = norm_rows(embedded, layer_gain)
    partial_pre = jnp.dot(
        lax.all_gather(normed, "col", axis=0, tiled=True),
        in_weight,
        preferred_element_type=jnp.float32,
    )
    pre_share = lax.psum_scatter(partial_pre, "row", scatter_dimension=0, tiled=True) + in_bias
    hidden = jax.nn.gelu(pre_share, approximate=False).astype(jnp.bfloat16)
    partial_branch = jnp.dot(
        lax.all_gather(hidden, "row", axis=0, tiled=True),
        out_weight,
        preferred_element_type=jnp.float32,
    )
    updated = (
        embedded
        + lax.psum_scatter(partial_branch, "col", scatter_dimension=0, tiled=True)
        + out_bias
    )
    final_normed = norm_rows(updated, final_gain)
    check_logits = lax.psum(
        jnp.dot(final_normed, check_weight, preferred_element_type=jnp.float32), "row"
    )
    return (in_weight, out_weight, check_logits)


def solution(mesh):
    placed = (
        P(("rep", "col"), None),
        P(None, "row"),
        P("row"),
        P(("row", "col"), None, None),
        P(("row", "col"), None, None),
        P(),
        P(None, "row"),
        P(None, "col"),
        P(None, "row"),
        P("row"),
        P("row", None),
    )
    return jax.shard_map(
        on_device,
        mesh=mesh,
        in_specs=placed,
        out_specs=(P("row", "col"), P("col", "row"), P(("rep", "col"), None)),
        check_vma=False,
    )
```

profile of v0, /device:TPU:0, one launch (start us, length us, event | category | flops | bytes accessed | tf_op | source)
XLA Modules:
  0.0 1160.1 jit_solution(9391864358575194546)
XLA Ops:
  7.2 0.0 copy-start
  7.2 0.0 all-gather.3.cloned.1.call-start
  7.2 10.0 copy.15
  17.2 0.0 copy-start.2
  17.2 0.0 copy-start.8
  17.2 0.0 copy-start.9
  17.2 4.0 broadcast_select_fusion.2
  21.3 5.6 copy-done.2
  26.9 3.0 collective-permute-start
  30.5 3.2 fusion.22
  33.7 11.9 %all-reduce.1 = (f32[512]{0:T(512)S(1)}, f32[512]{0:T(512)S(1)}) all-reduce(f32[512]{0:T(512)S(1)} %get-tuple-element.6, f32[512]{0:T(512)S(1)} %get-tuple-element.5), channel_id=1, replica_groups=mesh['rep'=4,'row'=4,'col'=2] {'row'}, use_global_device_ids=true, to_apply=%region_3.4 | all-reduce | flops 1024 | bytes 8192 | tf_op jit(solution)/shard_map/psum | solution.py:28
  45.7 0.0 copy-done.5
  45.7 0.2 convolution_reduce_fusion.1
  45.9 3.6 multiply_convert_fusion.1
  49.5 0.0 all-gather.3.cloned.1.call-update
  49.5 0.0 reduce-scatter.3.cloned.1.call-start
  49.6 217.2 %collective-permute-done = bf16[768,6144]{1,0:T(8,128)(2,1)} collective-permute-done((bf16[768,6144]{1,0:T(8,128)(2,1)}, bf16[768,6144]{1,0:T(8,128)(2,1)}, u32[]{:S(2)}, u32[]{:S(2)}) %collective-permute-start) | collective-permute-done | bytes 9437216 | tf_op jit(solution)/shard_map/ppermute | solution.py:16
  266.8 9.7 broadcast_select_fusion.1
  276.5 21.6 %pad_maximum_fusion = bf16[1536,6144]{1,0:T(8,128)(2,1)} fusion(bf16[768,6144]{1,0:T(8,128)(2,1)S(1)} %get-tuple-element.13, bf16[768,6144]{1,0:T(8,128)(2,1)S(1)} %get-tuple-element.12), kind=kLoop, calls=%fused_computation | loop fusion | flops 37748736 | bytes 37748736 | tf_op jit(solution)/shard_map/concatenate | solution.py:89
  298.1 26.1 %fusion.24 = f32[1024,6144]{1,0:T(8,128)} fusion(bf16[1024,1536]{1,0:T(8,128)(2,1)} %all-gather.3.cloned.1.call-done, bf16[1536,6144]{1,0:T(8,128)(2,1)} %pad_maximum_fusion), kind=kOutput, calls=%fused_computation.54 | convolution fusion | flops 19327352832 | bytes 47185920 | tf_op jit(solution)/shard_map/dot_general | solution.py:96
  324.3 0.0 reduce-scatter.3.cloned.1.call-update
  324.3 0.0 all-gather.5.cloned.1.call-start
  324.3 1.2 copy-done.3
  325.5 0.5 fusion.15
  326.0 414.1 %reduce-scatter.3.cloned.1.call-done = f32[256,6144]{1,0:T(8,128)} async-done(((f32[1024,6144]{1,0:T(8,128)}), f32[256,6144]{1,0:T(8,128)}) %reduce-scatter.3.cloned.1.call-update) | async-done | bytes 6291472 | tf_op jit(solution)/shard_map/reduce_scatter | solution.py:101
  740.1 15.9 %fusion.2 = bf16[256,6144]{1,0:T(8,128)(2,1)} fusion(f32[256,6144]{1,0:T(8,128)} %reduce-scatter.3.cloned.1.call-done, f32[6144]{0:T(1024)S(1)} %bitcast.36), kind=kLoop, calls=%fused_computation.11 | loop fusion | flops 103809024 | bytes 9461760 | tf_op jit(solution)/shard_map/convert_element_type | solution.py:102
  756.0 0.0 all-gather.5.cloned.1.call-update
  756.0 0.2 reduce-scatter.5.cloned.1.call-start
  756.3 7.5 fusion.23
  763.8 1.1 bitcast_select_fusion.1
  764.8 1.5 collective-permute-start.1
  766.4 203.3 %collective-permute-done.1 = bf16[6144,768]{1,0:T(8,128)(2,1)} collective-permute-done((bf16[6144,768]{1,0:T(8,128)(2,1)S(1)}, bf16[6144,768]{1,0:T(8,128)(2,1)}, u32[]{:S(2)}, u32[]{:S(2)}) %collective-permute-start.1) | collective-permute-done | bytes 9437216 | tf_op jit(solution)/shard_map/ppermute | solution.py:16
  969.7 9.6 bitcast_select_fusion.2
  979.3 14.5 %pad_maximum_fusion.1 = bf16[6144,1536]{1,0:T(8,128)(2,1)} fusion(bf16[6144,768]{1,0:T(8,128)(2,1)} %get-tuple-element.17, bf16[6144,768]{1,0:T(8,128)(2,1)S(1)} %get-tuple-element.16), kind=kLoop, calls=%fused_computation.1 | loop fusion | flops 37748736 | bytes 37748736 | tf_op jit(solution)/shard_map/concatenate | solution.py:90
  993.8 26.1 %fusion.25 = f32[1024,1536]{1,0:T(8,128)} fusion(bf16[1024,6144]{1,0:T(8,128)(2,1)} %all-gather.5.cloned.1.call-done, bf16[6144,1536]{1,0:T(8,128)(2,1)} %pad_maximum_fusion.1), kind=kOutput, calls=%fused_computation.55 | convolution fusion | flops 19327352832 | bytes 37748736 | tf_op jit(solution)/shard_map/dot_general | solution.py:103
  1019.9 0.0 reduce-scatter.5.cloned.1.call-update
  1020.0 0.0 copy-start.4
  1020.0 0.0 copy-start.7
  1020.0 0.0 all-reduce.4.cloned.1.call-start
  1020.0 0.9 copy-done.6
  1020.9 0.2 convolution_reduce_fusion
  1021.1 78.1 %reduce-scatter.5.cloned.1.call-done = f32[512,1536]{1,0:T(8,128)} async-done(((f32[1024,1536]{1,0:T(8,128)}), f32[512,1536]{1,0:T(8,128)}) %reduce-scatter.5.cloned.1.call-update) | async-done | bytes 3145744 | tf_op jit(solution)/shard_map/reduce_scatter | solution.py:110
  1099.2 4.8 fusion.21
  1104.0 11.7 %all-reduce = (f32[512]{0:T(512)S(1)}, f32[512]{0:T(512)S(1)}) all-reduce(f32[512]{0:T(512)S(1)} %get-tuple-element.4, f32[512]{0:T(512)S(1)} %get-tuple-element.3), channel_id=1, replica_groups=mesh['rep'=4,'row'=4,'col'=2] {'row'}, use_global_device_ids=true, to_apply=%region_9.10 | all-reduce | flops 1024 | bytes 8192 | tf_op jit(solution)/shard_map/psum | solution.py:28
  1115.7 3.2 fusion.10
  1118.9 0.0 all-reduce.4.cloned.1.call-update
  1119.0 33.0 %all-reduce.4.cloned.1.call-done = f32[512,128]{1,0:T(8,128)} async-done(((f32[512,128]{1,0:T(8,128)}), f32[512,128]{1,0:T(8,128)}) %all-reduce.4.cloned.1.call-update) | async-done | bytes 262160 | tf_op jit(solution)/shard_map/psum | solution.py:114
  1151.9 1.7 copy.18
  (14 shorter events, 0.0 us)
Async XLA Ops:
  7.2 23.3 %copy-start = (bf16[588,1536]{1,0:T(8,128)(2,1)S(1)}, bf16[588,1536]{1,0:T(8,128)(2,1)}, u32[]{:S(2)}) copy-start(bf16[588,1536]{1,0:T(8,128)(2,1)} %param.12) | copy-start | bytes 5419012
  7.2 291.0 %all-gather.3.cloned.1.call-start = ((), (), s32[]{:S(2)}) async-start(), calls=%async_computation.2 | async-start | bytes 4718592 | tf_op jit(solution)/shard_map/all_gather | solution.py:97
  17.2 9.7 copy-start.2
  17.2 13.3 %copy-start.8 = (bf16[512,588]{0,1:T(8,128)(2,1)S(1)}, bf16[512,588]{0,1:T(8,128)(2,1)}, u32[]{:S(2)}) copy-start(bf16[512,588]{0,1:T(8,128)(2,1)} %param.11) | copy-start | bytes 1806340
  17.2 13.3 %copy-start.9 = (f32[1536]{0:T(1024)S(1)}, f32[1536]{0:T(1024)}, u32[]{:S(2)}) copy-start(f32[1536]{0:T(1024)} %param.13) | copy-start | bytes 18436
  26.9 18.8 %copy-start.5 = (f32[48,1536]{1,0:T(8,128)S(1)}, f32[48,1536]{1,0:T(8,128)}, u32[]{:S(2)}) copy-start(f32[48,1536]{1,0:T(8,128)} %param.17) | copy-start | bytes 884740
  26.9 239.9 %collective-permute-start = (bf16[768,6144]{1,0:T(8,128)(2,1)}, bf16[768,6144]{1,0:T(8,128)(2,1)}, u32[]{:S(2)}, u32[]{:S(2)}) collective-permute-start(bf16[768,6144]{1,0:T(8,128)(2,1)} %broadcast_select_fusion.2), channel_id=1, source_target_pairs={{0,1},{1,0},{2,3},{3,2},{4,5},{5,4},{6,7},{7,6},{8,9},{9,8},{10,11... | collective-permute-start | bytes 28311560 | tf_op jit(solution)/shard_map/ppermute | solution.py:16
  49.5 690.6 %reduce-scatter.3.cloned.1.call-start = ((), (), s32[]{:S(2)}) async-start(), calls=%async_computation.3 | async-start | bytes 31457280 | tf_op jit(solution)/shard_map/reduce_scatter | solution.py:101
  324.3 1.3 copy-start.3
  324.3 669.5 %all-gather.5.cloned.1.call-start = ((), (), s32[]{:S(2)}) async-start(), calls=%async_computation.4 | async-start | bytes 15728640 | tf_op jit(solution)/shard_map/all_gather | solution.py:104
  756.0 343.1 %reduce-scatter.5.cloned.1.call-start = ((), (), s32[]{:S(2)}) async-start(), calls=%async_computation.5 | async-start | bytes 9437184 | tf_op jit(solution)/shard_map/reduce_scatter | solution.py:110
  764.8 204.9 %collective-permute-start.1 = (bf16[6144,768]{1,0:T(8,128)(2,1)S(1)}, bf16[6144,768]{1,0:T(8,128)(2,1)}, u32[]{:S(2)}, u32[]{:S(2)}) collective-permute-start(bf16[6144,768]{1,0:T(8,128)(2,1)S(1)} %bitcast_select_fusion.1), channel_id=1, source_target_pairs={{0,1},{1,0},{2,3},{3,2},{4,5},{5,4},{6,7},{7,6},{8,9},{9,8},{10,11... | collective-permute-start | bytes 28311560 | tf_op jit(solution)/shard_map/ppermute | solution.py:16
  1019.9 1.0 copy-start.6
  1020.0 95.8 %copy-start.4 = (bf16[1536,128]{1,0:T(8,128)(2,1)S(1)}, bf16[1536,128]{1,0:T(8,128)(2,1)}, u32[]{:S(2)}) copy-start(bf16[1536,128]{1,0:T(8,128)(2,1)} %param.21) | copy-start | bytes 1179652
  1020.0 95.7 %copy-start.7 = (f32[1536]{0:T(1024)S(1)}, f32[1536]{0:T(1024)}, u32[]{:S(2)}) copy-start(f32[1536]{0:T(1024)} %param.20) | copy-start | bytes 18436
  1020.0 132.0 %all-reduce.4.cloned.1.call-start = ((), (), s32[]{:S(2)}) async-start(), calls=%async_computation.6 | async-start | bytes 524288 | tf_op jit(solution)/shard_map/psum | solution.py:114
  1020.9 132.7 %copy-start.1 = (bf16[588,1536]{1,0:T(8,128)(2,1)S(1)}, bf16[588,1536]{1,0:T(8,128)(2,1)}, u32[]{:S(2)}) copy-start(bf16[588,1536]{1,0:T(8,128)(2,1)} %param.12) | copy-start | bytes 5419012
Sparse Core Ops, SparseCore 0:
  49.6 75.9 all-gather.2
  324.4 415.6 reduce-scatter.2
  756.2 220.1 all-gather.4
  1020.1 79.0 reduce-scatter.4
  1119.1 32.8 all-reduce.3
where the time goes:
time: 1160 us
  waiting for transfers between devices  946 us (82%)
  other arithmetic  84.8 us (7%)
  matrix products  59.6 us (5%)
  local copies, waits for them, and re-layouts  26.9 us (2%)
  blocking collectives  23.6 us (2%)
  between operations  14.6 us (1%)
    ppermute x2, waiting for transfers between devices, partner(): return lax.ppermute(value, axis, pairs)  421 us
    reduce_scatter x1, waiting for transfers between devices, on_device(): lax.psum_scatter(partial_pre, 'row', scatter_dimension=0, tiled=True)  414 us
    reduce_scatter x1, waiting for transfers between devices, on_device(): lax.psum_scatter(partial_branch, 'col', scatter_dimension=0, tiled=True)  78.1 us
    psum x1, waiting for transfers between devices, on_device(): lax.psum(jnp.dot(final_normed, check_weight, preferred_element_type=jnp.f...  33 us
    dot_general x1, matrix products, on_device(): jnp.dot(lax.all_gather(hidden, 'row', axis=0, tiled=True), out_weight, pr...  26.1 us
    dot_general x1, matrix products, on_device(): jnp.dot(lax.all_gather(normed, 'col', axis=0, tiled=True), in_weight, pre...  26.1 us
    psum x2, blocking collectives, norm_rows(): lax.psum((jnp.sum(values, axis=1), jnp.sum(values * values, axis=1)), 'row')  23.6 us
  transfers between devices with their start and end apart: 7, of which 5 were waited for; matrix products, arithmetic and copies ran while one was open for 6% of the time, Pallas kernels for 0%

commit v1 on v0

v1 whole, which is shorter than its diff:
```python
import functools

import jax
import jax.numpy as jnp
from jax import lax
from jax.experimental import pallas as pl
from jax.experimental.pallas import tpu as pltpu
from jax.sharding import PartitionSpec as P


EPSILON = 1e-06


def swap(value, axis, mask):
    pairs = [(source, source ^ mask) for source in range(lax.axis_size(axis))]
    return lax.ppermute(value, axis, pairs)


def masks(axis):
    return [2**bit for bit in range(lax.axis_size(axis).bit_length() - 1)]


def all_sum(value, axis):
    for mask in masks(axis):
        value = value + swap(value, axis, mask)
    return value


def gather_xor(value, axis):
    for mask in masks(axis):
        value = jnp.concatenate([value, swap(value, axis, mask)], axis=0)
    return value


def scatter_xor(value, axis):
    for mask in reversed(masks(axis)):
        half = value.shape[0] // 2
        value = value[:half] + swap(value[half:].astype(jnp.bfloat16), axis, mask).astype(jnp.float32)
    return value


def row_of(table, restore_id):
    return lax.dynamic_index_in_dim(table, restore_id[0], 0, keepdims=False)


def through(moves, buffers, arrive, leave):
    reads, writes = [], []
    for n, ((source, target), buffer) in enumerate(zip(moves, buffers)):
        reads.append(pltpu.make_async_copy(source, buffer, arrive.at[n]))
        writes.append(pltpu.make_async_copy(buffer, target, leave.at[n]))
    for read in reads:
        read.start()
    for read, write in zip(reads, writes):
        read.wait()
        write.start()
    for write in writes:
        write.wait()


def copy_cost(size):
    return pl.CostEstimate(flops=300 * size, transcendentals=0, bytes_accessed=2 * size)


def block_at(ref, row, row_size, column, column_size):
    return ref.at[pl.ds(pl.multiple_of(row, row_size), row_size), pl.ds(pl.multiple_of(column, column_size), column_size)]


def keep_body(place_ref, old_in, old_out, in_ref, out_ref, in_buffer, out_buffer, arrive, leave, *, kept):
    col = place_ref[2]
    _, tile_rows, tile_cols = old_in.shape
    moves, buffers = [], []
    for j in range(kept):
        target = block_at(in_ref, col * tile_rows, tile_rows, j * tile_cols, tile_cols)
        moves.append((old_in.at[col * kept + j], target))
        buffers.append(in_buffer.at[j])
    for j in range(kept):
        target = block_at(out_ref, j * tile_cols, tile_cols, col * tile_rows, tile_rows)
        moves.append((old_out.at[col * kept + j], target))
        buffers.append(out_buffer.at[j])
    through(moves, buffers, arrive, leave)


def keep_tiles(place, old_in, old_out):
    count, tile_rows, tile_cols = old_in.shape
    kept = count // 2
    hbm = pl.BlockSpec(memory_space=pl.ANY)
    kind = old_in.dtype
    return pl.pallas_call(
        functools.partial(keep_body, kept=kept),
        in_specs=[pl.BlockSpec(memory_space=pltpu.SMEM), hbm, hbm],
        out_specs=[hbm] * 2,
        out_shape=[
            jax.ShapeDtypeStruct((2 * tile_rows, kept * tile_cols), kind),
            jax.ShapeDtypeStruct((kept * tile_cols, 2 * tile_rows), kind),
        ],
        scratch_shapes=[
            pltpu.VMEM((kept, tile_rows, tile_cols), kind),
            pltpu.VMEM((kept, tile_cols, tile_rows), kind),
            pltpu.SemaphoreType.DMA((2 * kept,)),
            pltpu.SemaphoreType.DMA((2 * kept,)),
        ],
        cost_estimate=copy_cost(4 * kept * tile_rows * tile_cols),
        name="keep_tiles",
    )(place, old_in, old_out)


def fill_in_body(place_ref, *refs, parts, counts, rows):
    weight, (buffer, arrive, leave) = refs[-4], refs[-3:]
    rep, row, col = (place_ref[n] for n in range(3))
    moves, buffers, n = [], [], 0
    for k in range(parts):
        first = 0
        for m, count in enumerate(counts):
            part = refs[m * parts + k]
            _, tile_rows, width = part.shape
            for i in range(count):
                column = ((rep ^ k) * rows + (row ^ (first + i))) * width
                target = block_at(weight, (1 - col) * tile_rows, tile_rows, column, width)
                moves.append((part.at[i], target))
                buffers.append(buffer.at[n])
                n += 1
            first += count
    through(moves, buffers, arrive, leave)


def fill(place, parts, weight, body, pieces):
    hbm = pl.BlockSpec(memory_space=pl.ANY)
    return pl.pallas_call(
        body,
        in_specs=[pl.BlockSpec(memory_space=pltpu.SMEM)] + [hbm] * (len(parts) + 1),
        out_specs=hbm,
        out_shape=jax.ShapeDtypeStruct(weight.shape, weight.dtype),
        scratch_shapes=[
            pltpu.VMEM((pieces,) + parts[0].shape[1:], weight.dtype),
            pltpu.SemaphoreType.DMA((pieces,)),
            pltpu.SemaphoreType.DMA((pieces,)),
        ],
        input_output_aliases={1 + len(parts): 0},
        cost_estimate=copy_cost(2 * sum(part.size for part in parts)),
    )(place, *parts, weight)


def cut_body(place_ref, tile_ref, *out_refs):
    row, width = place_ref[1], out_refs[0].shape[-1]
    n = 0
    for ref in out_refs:
        for i in range(ref.shape[0]):
            start = pl.multiple_of((row ^ n) * width, width)
            ref[i] = tile_ref[0, :, pl.ds(start, width)]
            n += 1


def cut_tile(tiles, which, row, counts):
    _, tile_rows, tile_cols = tiles.shape
    width = tile_cols // sum(counts)
    spec = pltpu.PrefetchScalarGridSpec(
        num_scalar_prefetch=1,
        grid=(1,),
        in_specs=[pl.BlockSpec((1, tile_rows, tile_cols), lambda i, s: (s[0], 0, 0))],
        out_specs=[pl.BlockSpec((count, tile_rows, width), lambda i, s: (0, 0, 0)) for count in counts],
    )
    return pl.pallas_call(
        cut_body,
        grid_spec=spec,
        out_shape=[jax.ShapeDtypeStruct((count, tile_rows, width), tiles.dtype) for count in counts],
        name="cut_tile",
    )(jnp.stack([which, row]).astype(jnp.int32), tiles)


def spread(part, axis):
    parts = {0: part}
    for mask in reversed(masks(axis)):
        for k in sorted(parts):
            parts[k ^ mask] = swap(parts[k], axis, mask)
    return [parts[k] for k in sorted(parts)]


def layer_body(place_ref, tokens_ref, scale_ref, bias_ref, tile_ref, *refs, groups, adds):
    pieces = [ref.at[i] for ref in refs[:groups] for i in range(ref.shape[0])]
    sum_ref, hidden_ref = refs[-2:]
    row, width = place_ref[1], pieces[0].shape[-1]
    tokens = tokens_ref[...]
    total = refs[groups][...] if adds else None
    for j, piece in enumerate(pieces):
        start = pl.multiple_of((row ^ j) * width, width)
        pre = jnp.dot(tokens, piece[...], preferred_element_type=jnp.float32)
        pre = pre * scale_ref[...] + bias_ref[row ^ j]
        half = 0.5 * pre
        hidden = (half + half * lax.erf(pre * (0.5**0.5))).astype(jnp.bfloat16)
        hidden_ref[:, pl.ds(start, width)] = hidden
        term = jnp.dot(hidden, tile_ref[0, pl.ds(start, width), :], preferred_element_type=jnp.float32)
        total = term if total is None else total + term
    sum_ref[...] = total


def came_body(place_ref, *refs, first, shares, halves, fills):
    value_refs, part_refs = refs[:shares], refs[shares : shares * (1 + halves)]
    refs = refs[shares * (1 + halves) + fills :]
    sum_ref, refs = refs[0], refs[1:]
    weight, refs = (refs[0], refs[1:]) if fills else (None, refs)
    values, parts, arrive, leave, total = refs
    rep, col = place_ref[0], place_ref[2]
    count, width = values.shape[1:]
    height, features = parts.shape[1] // halves, parts.shape[2]
    reads = []
    for k in range(shares):
        group = [pltpu.make_async_copy(value_refs[k].at[pl.ds(first, count)], values.at[k], arrive.at[k, 0])]
        for h in range(halves):
            group.append(
                pltpu.make_async_copy(
                    part_refs[k * halves + h].at[0], parts.at[k, pl.ds(h * height, height)], arrive.at[k, 1 + h]
                )
            )
        for copy in group:
            copy.start()
        reads.append(group)
    writes = []
    for k in range(shares):
        for copy in reads[k]:
            copy.wait()
        if fills:
            target = block_at(weight, (rep ^ k) * width, width, (1 - col) * features, features)
            writes.append(pltpu.make_async_copy(parts.at[k], target, leave.at[k]))
            writes[-1].start()
        term = jnp.dot(values[k], parts[k], preferred_element_type=jnp.float32)
        if k == 0:
            total[...] = term
        elif k < shares - 1:
            total[...] += term
        else:
            sum_ref[...] = (total[...] + term).astype(sum_ref.dtype)
    for copy in writes:
        copy.wait()


def came_sum(place, values, parts, first, count, kind, weight):
    shares, halves = len(values), len(parts) // len(values)
    width, features = values[0].shape[1], parts[0].shape[2]
    hbm = pl.BlockSpec(memory_space=pl.ANY)
    fills = weight is not None
    outs = [jax.ShapeDtypeStruct((count, features), kind)]
    return pl.pallas_call(
        functools.partial(came_body, first=first, shares=shares, halves=halves, fills=int(fills)),
        in_specs=[pl.BlockSpec(memory_space=pltpu.SMEM)] + [hbm] * (len(values) + len(parts) + fills),
        out_specs=[pl.BlockSpec(memory_space=pltpu.VMEM)] + [hbm] * fills,
        out_shape=outs + ([jax.ShapeDtypeStruct(weight.shape, weight.dtype)] if fills else []),
        scratch_shapes=[
            pltpu.VMEM((shares, count, width), values[0].dtype),
            pltpu.VMEM((shares, width, features), parts[0].dtype),
            pltpu.SemaphoreType.DMA((shares, 1 + halves)),
            pltpu.SemaphoreType.DMA((shares,)),
            pltpu.VMEM((count, features), jnp.float32),
        ],
        input_output_aliases={1 + len(values) + len(parts): 1} if fills else {},
        cost_estimate=pl.CostEstimate(
            flops=2 * count * shares * width * features,
            transcendentals=0,
            bytes_accessed=2 * shares * width * (count + features),
        ),
        name="came_sum",
    )(place, *values, *parts, *((weight,) if fills else ()))


def layer_share(place, tokens, scale, bias, tiles, pieces, total, block):
    count, depth = tokens.shape
    _, tile_rows, tile_cols = tiles.shape
    spec = pltpu.PrefetchScalarGridSpec(
        num_scalar_prefetch=1,
        grid=(count // block,),
        in_specs=[
            pl.BlockSpec((block, depth), lambda i, s: (i, 0)),
            pl.BlockSpec((block, 1), lambda i, s: (i, 0)),
            pl.BlockSpec(bias.shape, lambda i, s: (0, 0, 0)),
            pl.BlockSpec((1, tile_rows, tile_cols), lambda i, s: (s[0], 0, 0)),
        ]
        + [pl.BlockSpec(piece.shape, lambda i, s: (0, 0, 0)) for piece in pieces]
        + ([] if total is None else [pl.BlockSpec((block, tile_cols), lambda i, s: (i, 0))]),
        out_specs=[
            pl.BlockSpec((block, tile_cols), lambda i, s: (i, 0)),
            pl.BlockSpec((block, tile_rows), lambda i, s: (i, 0)),
        ],
    )
    return pl.pallas_call(
        functools.partial(layer_body, groups=len(pieces), adds=total is not None),
        grid_spec=spec,
        out_shape=[
            jax.ShapeDtypeStruct((count, tile_cols), jnp.float32),
            jax.ShapeDtypeStruct((count, tile_rows), jnp.bfloat16),
        ],
        input_output_aliases={} if total is None else {5 + len(pieces): 0},
        cost_estimate=pl.CostEstimate(
            flops=2 * count * tile_rows * (depth + tile_cols),
            transcendentals=count * tile_rows,
            bytes_accessed=2 * tile_rows * (tile_cols + depth) + count * (8 * tile_cols + 2 * tile_rows),
        ),
        name="layer_share",
    )(place, tokens, scale, bias, tiles, *pieces, *(() if total is None else (total,)))


def move_halves(pieces, axis):
    index = lax.axis_index(axis)
    for bit, mask in enumerate(masks(axis)):
        upper_side = index >> bit & 1 == 1
        outgoing = tuple(jnp.where(upper_side, low, high) for low, high in pieces)
        incoming = tuple(swap(part, axis, mask) for part in outgoing)
        pieces = tuple(
            (jnp.where(upper_side, came, low), jnp.where(upper_side, high, came))
            for (low, high), came in zip(pieces, incoming)
        )
    return pieces


def relayout_any(old_in, old_out):
    tiles_here, tile_rows, tile_cols = old_in.shape
    local_cols = tiles_here * tile_cols
    half = local_cols // 2
    in_local = jnp.transpose(old_in, (1, 0, 2)).reshape(tile_rows, local_cols)
    out_local = old_out.reshape(local_cols, tile_rows)
    in_pair, out_pair = move_halves(
        ((in_local[:, :half], in_local[:, half:]), (out_local[:half], out_local[half:])), "col"
    )
    return jnp.concatenate(in_pair, axis=0), jnp.concatenate(out_pair, axis=1)


def on_device(
    patches,
    embed_weight,
    embed_bias,
    old_in,
    old_out,
    restore_id,
    norm_gains,
    in_biases,
    out_biases,
    final_gain,
    check_weight,
):
    reps, rows, cols = (lax.axis_size(axis) for axis in ("rep", "row", "col"))
    rep, row, col = (lax.axis_index(axis) for axis in ("rep", "row", "col"))
    tiles_here, tile_rows, tile_cols = old_in.shape
    tokens, patch = patches.shape
    features = embed_weight.shape[1]
    feature_count = features * rows
    depth = -(-(patch + 1) // 16) * 16
    pair = cols == 2 and reps == 4 and tiles_here == 2 * reps and features == 2 * tile_rows and tile_cols % (128 * rows) == 0

    if pair:
        kept = tiles_here // 2
        own, away = col * kept, (1 - col) * kept
        cut = [rows // 2, rows - rows // 2]
        in_sent = cut_tile(old_in, away + rep, row, cut)
        in_sent, embed_weight, embed_bias, patches = lax.optimization_barrier(
            (in_sent, embed_weight, embed_bias, patches)
        )
        in_came = [None] * len(cut)
        for m in reversed(range(len(cut))):
            in_came[m] = swap(in_sent[m], "col", 1)
        in_mine = cut_tile(old_in, own + rep, row, cut)
        where = jnp.stack([rep, row, col]).astype(jnp.int32)
        in_weight, out_weight = keep_tiles(where, old_in, old_out)
    else:
        in_weight, out_weight = relayout_any(old_in, old_out)

    def mine_first(values, axis):
        return jnp.roll(values, -col * tile_rows, axis) if pair else values

    layer_gain = mine_first(row_of(norm_gains, restore_id), 0)
    in_bias = row_of(in_biases, restore_id)
    out_bias = mine_first(row_of(out_biases, restore_id), 0)
    embed_weight = mine_first(embed_weight, 1)
    embed_bias = mine_first(embed_bias, 0)
    final_gain = mine_first(final_gain, 0)
    check_weight = mine_first(check_weight, 0)

    embedded = jnp.dot(patches, embed_weight, preferred_element_type=jnp.float32) + embed_bias
    weight_f32 = embed_weight.astype(jnp.float32)
    sums = all_sum(
        jnp.concatenate(
            [
                jnp.sum(embedded, axis=1),
                jnp.sum(embedded * embedded, axis=1),
                jnp.sum(weight_f32, axis=1),
                jnp.sum(embed_bias)[None],
            ]
        ),
        "row",
    ) / feature_count
    one, late, sums = lax.optimization_barrier((jnp.ones((tokens, 1), patches.dtype), (1 - col) * (tiles_here // 2), sums))
    tokens_in = jnp.concatenate(
        [patches, one, jnp.zeros((tokens, depth - patch - 1), patches.dtype)], axis=1
    )
    tokens_in = gather_xor(tokens_in, "col")
    if pair:
        height = tile_cols // 2

        def out_half(k, half):
            sent = lax.dynamic_slice(old_out, (late + (rep ^ k), half * height, 0), (1, height, tile_rows))
            return swap(sent, "col", 1)

        out_parts = {(0, 0): out_half(0, 0), (0, 1): out_half(0, 1), (2, 1): out_half(2, 1)}

    average, square = sums[:tokens], sums[tokens : 2 * tokens]
    scale = gather_xor(lax.rsqrt(square - average * average + EPSILON), "col")[:, None]

    centers = sums[2 * tokens :]
    centered = jnp.concatenate(
        [
            (weight_f32 - centers[:patch, None]) * layer_gain,
            ((embed_bias - centers[patch]) * layer_gain)[None],
            jnp.zeros((depth - patch - 1, features), jnp.float32),
        ]
    ).astype(jnp.bfloat16)
    hidden_here = in_weight.shape[1]
    share = hidden_here // reps
    piece = share // rows

    def times(left, right):
        return jnp.dot(left, right, preferred_element_type=jnp.float32)

    def partial(k):
        if not pair:
            return times(centered, lax.dynamic_slice_in_dim(in_weight, rep * share + (row ^ k) * piece, piece, 1))
        m, i = (0, k) if k < cut[0] else (1, k - cut[0])
        return times(centered[:, :tile_rows], in_mine[m][i]) + times(centered[:, tile_rows:], in_came[m][i])

    came = [swap(partial(k).astype(jnp.bfloat16), "row", k) for k in reversed(range(1, rows))]
    folded = partial(0)
    for value in came:
        folded = folded + value.astype(jnp.float32)
    folded = folded.astype(jnp.bfloat16)
    group = spread(folded, "row")

    if pair:
        groups = {0: group}
        for mask in reversed(masks("rep")):
            for k in sorted(groups):
                if mask > 1:
                    groups[k ^ mask] = [swap(value, "rep", mask) for value in groups[k]]
                else:
                    groups[k ^ mask] = [swap(jnp.stack(groups[k]), "rep", mask)]
        in_parts = [spread(part, "rep") for part in in_came]
        out_parts[2, 0] = swap(out_parts[0, 0], "rep", 2)
        for k, half in sorted(out_parts):
            out_parts[k ^ 1, half] = swap(out_parts[k, half], "rep", 1)
        in_weight = fill(
            where,
            [part for parts in in_parts for part in parts],
            in_weight,
            functools.partial(fill_in_body, parts=reps, counts=cut, rows=rows),
            reps * rows,
        )
        biases = in_bias.reshape(reps, rows, 1, piece)
        branch_mine = None
        order = sorted(groups, key=lambda k: (bin(k).count("1"), k))
        values = {}
        for k in order:
            pieces = [value if value.ndim == 3 else value[None] for value in groups[k]]
            place = jnp.stack([own + (rep ^ k), row]).astype(jnp.int32)
            bias = lax.dynamic_index_in_dim(biases, rep ^ k, 0, keepdims=False)
            branch_mine, values[k] = layer_share(
                place, tokens_in, scale, bias, old_out, pieces, branch_mine, min(256, tokens_in.shape[0])
            )

        shares = [values[k] for k in sorted(values)]
        parts = [out_parts[key] for key in sorted(out_parts)]
        to_came = swap(branch_mine[tokens:].astype(jnp.bfloat16), "col", 1).astype(jnp.float32)
        theirs, out_weight = came_sum(where, shares, parts, tokens, tokens, jnp.bfloat16, out_weight)
        to_mine = swap(theirs, "col", 1).astype(jnp.float32)
        (branch_came,) = came_sum(where, shares, parts, 0, tokens, jnp.float32, None)
        branch = jnp.concatenate([branch_mine[:tokens] + to_mine, branch_came + to_came], axis=1)
    else:
        group = jnp.take(jnp.stack(group), row ^ jnp.arange(rows), axis=0)
        shares = jnp.take(jnp.stack(spread(group, "rep")), rep ^ jnp.arange(reps), axis=0)
        folded = jnp.transpose(shares, (2, 0, 1, 3)).reshape(depth, hidden_here)
        pre = times(tokens_in, folded) * scale + in_bias
        hidden = (0.5 * pre * (1.0 + lax.erf(pre * (0.5**0.5)))).astype(jnp.bfloat16)
        branch = scatter_xor(times(hidden, out_weight), "col")
    updated = embedded + branch + out_bias

    center = jnp.mean(updated, axis=1, keepdims=True)
    weighted = final_gain[:, None] * check_weight.astype(jnp.float32)
    slope = jnp.sum(weighted, axis=0, keepdims=True)
    logits = times(((updated - center) * final_gain).astype(jnp.bfloat16), check_weight) + center * slope
    checks = logits.shape[1]
    moments = jnp.concatenate([jnp.sum(updated, axis=1), jnp.sum(updated * updated, axis=1), slope[0]])
    moments = jnp.pad(moments, (0, -moments.size % (8 * checks))).reshape(-1, checks)
    total = all_sum(jnp.concatenate([logits, moments]), "row")
    moments = total[tokens:].reshape(-1)
    average = moments[:tokens, None] / feature_count
    variance = moments[tokens : 2 * tokens, None] / feature_count - average * average
    slope = moments[None, 2 * tokens : 2 * tokens + checks]
    check_logits = (total[:tokens] - average * slope) * lax.rsqrt(variance + EPSILON)
    return (in_weight, out_weight, check_logits)


def solution(mesh):
    placed = (
        P(("rep", "col"), None),
        P(None, "row"),
        P("row"),
        P(("row", "col"), None, None),
        P(("row", "col"), None, None),
        P(),
        P(None, "row"),
        P(None, "col"),
        P(None, "row"),
        P("row"),
        P("row", None),
    )
    return jax.shard_map(
        on_device,
        mesh=mesh,
        in_specs=placed,
        out_specs=(P("row", "col"), P("col", "row"), P(("rep", "col"), None)),
        check_vma=False,
    )
```

time: 1160 us -> 348 us (0.30)
  waiting for transfers between devices: 946 us -> 143 us
  Pallas kernels: 0 us -> 101 us
  other arithmetic: 84.8 us -> 24.3 us
  matrix products: 59.6 us -> 14.5 us
  starting transfers between devices: 4.9 us -> 43.5 us
  blocking collectives: 23.6 us -> 0 us
  between operations: 14.6 us -> 1.81 us
    reduce_scatter x2 -> x0, waiting for transfers between devices: 492 us -> none  [the longest x1 414 us: on_device(): lax.psum_scatter(partial_pre, 'row', scatter_dimension=0, tiled=True)]
    ppermute x2 -> x36, waiting for transfers between devices: 421 us -> 143 us  [swap(): return lax.ppermute(value, axis, pairs)]
    pallas_call x0 -> x10, Pallas kernels: none -> 101 us  [the longest x4 48.2 us: layer_share(): pl.pallas_call(functools.partial(layer_body, groups=len(pieces), adds=tot...]
    dot_general x6 -> x9, matrix products: 56.4 us -> 11.3 us  [times(): return jnp.dot(left, right, preferred_element_type=jnp.float32)]
    ppermute x2 -> x36, starting transfers between devices: 4.51 us -> 43.5 us  [swap(): return lax.ppermute(value, axis, pairs)]
    concatenate x2 -> x7, other arithmetic: 36.1 us -> 3.07 us  [the longest x2 2.37 us: gather_xor(): value = jnp.concatenate([value, swap(value, axis, mask)], axis=0)]
    psum x1 -> x0, waiting for transfers between devices: 33 us -> none  [on_device(): lax.psum(jnp.dot(final_normed, check_weight, preferred_element_type=jnp.f...]
    select_n x4 -> x0, other arithmetic: 24.4 us -> none  [the longest x2 19.3 us: move_halves(): jnp.where(upper_side, arrived, lower_part)]
  transfers between devices with their start and end apart: 7 -> 36, of which waited for: 5 -> 13; matrix products, arithmetic and copies ran while one was open for 6% -> 12% of each run, Pallas kernels for 0% -> 28%
where the time goes in v1:
time: 348 us; the launch traced here: 347 us
  waiting for transfers between devices  143 us (41%)
  Pallas kernels  101 us (29%)
  starting transfers between devices  43.5 us (12%)
  other arithmetic  24.3 us (7%)
  local copies, waits for them, and re-layouts  19.1 us (5%)
  matrix products  14.5 us (4%)
    ppermute x36, waiting for transfers between devices, swap(): return lax.ppermute(value, axis, pairs)  143 us
    pallas_call x4, Pallas kernels, layer_share(): pl.pallas_call(functools.partial(layer_body, groups=len(pieces), adds=tot...  48.2 us
    ppermute x36, starting transfers between devices, swap(): return lax.ppermute(value, axis, pairs)  43.5 us
    pallas_call x2, Pallas kernels, came_sum(): pl.pallas_call(functools.partial(came_body, first=first, shares=shares, h...  23.3 us
    pallas_call x1, Pallas kernels, keep_tiles(): pl.pallas_call(functools.partial(keep_body, kept=kept), in_specs=[pl.Bloc...  13.8 us
    dot_general x9, matrix products, times(): return jnp.dot(left, right, preferred_element_type=jnp.float32)  11.3 us
    pallas_call x1, Pallas kernels, fill(): pl.pallas_call(body, in_specs=[pl.BlockSpec(memory_space=pltpu.SMEM)] + [...  8.2 us
    pallas_call x2, Pallas kernels, cut_tile(): pl.pallas_call(cut_body, grid_spec=spec, out_shape=[jax.ShapeDtypeStruct(...  8.01 us
  transfers between devices with their start and end apart: 36, of which 13 were waited for; matrix products, arithmetic and copies ran while one was open for 12% of the time, Pallas kernels for 28%

profile of v1, /device:TPU:0, one launch (start us, length us, event | category | flops | bytes accessed | tf_op | source)
XLA Modules:
  0.0 347.2 jit_solution(16362935238565541665)
XLA Ops:
  1.3 4.1 %cut_tile.2 = (bf16[2,768,384]{2,1,0:T(8,128)(2,1)}, bf16[2,768,384]{2,1,0:T(8,128)(2,1)}) custom-call(s32[2]{0:T(128)} %pad_add_fusion.1.place_ref, bf16[8,768,1536]{2,1,0:T(8,128)(2,1)} %tile_ref.7), custom_call_target="tpu_custom_call" | custom-call | tf_op jit(solution)/shard_map/cut_tile/pallas_call | solution.py:162
  6.1 3.6 %convert_reduce_fusion = (f32[588]{0:T(1024)S(1)}, bf16[588,1536]{1,0:T(8,128)(2,1)S(1)}) fusion(s32[]{:T(128)S(6)} %select_n.54, bf16[588,1536]{1,0:T(8,128)(2,1)} %param.14), kind=kLoop, calls=%fused_computation.1 | loop fusion | flops 5418420 | bytes 3615028 | tf_op jit(solution)/shard_map/reduce_sum | solution.py:382
  9.7 3.2 multiply_reduce_fusion.1
  13.7 3.1 collective-permute-start.8
  18.8 2.6 collective-permute-start.9
  22.7 3.9 %cut_tile.3 = (bf16[2,768,384]{2,1,0:T(8,128)(2,1)}, bf16[2,768,384]{2,1,0:T(8,128)(2,1)}) custom-call(s32[2]{0:T(128)} %pad_add_fusion.2.place_ref, bf16[8,768,1536]{2,1,0:T(8,128)(2,1)} %tile_ref.7), custom_call_target="tpu_custom_call" | custom-call | tf_op jit(solution)/shard_map/cut_tile/pallas_call | solution.py:162
  33.2 12.7 %collective-permute-done.refs_0_ = bf16[2,768,384]{2,1,0:T(8,128)(2,1)} collective-permute-done((bf16[2,768,384]{2,1,0:T(8,128)(2,1)}, bf16[2,768,384]{2,1,0:T(8,128)(2,1)}, u32[]{:S(2)}, u32[]{:S(2)}) %collective-permute-start) | collective-permute-done | bytes 1179680 | tf_op jit(solution)/shard_map/ppermute | solution.py:16
  45.9 1.7 fusion.13
  47.8 22.0 %collective-permute-done.4.refs_4_ = bf16[2,768,384]{2,1,0:T(8,128)(2,1)} collective-permute-done((bf16[2,768,384]{2,1,0:T(8,128)(2,1)}, bf16[2,768,384]{2,1,0:T(8,128)(2,1)}, u32[]{:S(2)}, u32[]{:S(2)}) %collective-permute-start.4) | collective-permute-done | bytes 1179680 | tf_op jit(solution)/shard_map/ppermute | solution.py:16
  69.8 1.7 fusion.12
  71.5 2.7 collective-permute-start.13
  74.1 1.7 fusion.11
  76.7 26.4 %collective-permute-done.13 = bf16[592,384]{1,0:T(8,128)(2,1)S(1)} collective-permute-done((bf16[592,384]{1,0:T(8,128)(2,1)S(1)}, bf16[592,384]{1,0:T(8,128)(2,1)S(1)}, u32[]{:S(2)}, u32[]{:S(2)}) %collective-permute-start.13) | collective-permute-done | bytes 454688 | tf_op jit(solution)/shard_map/ppermute | solution.py:16
  103.1 1.8 fusion.10
  105.0 10.2 %collective-permute-start.15 = (bf16[592,384]{1,0:T(8,128)(2,1)S(1)}, bf16[592,384]{1,0:T(8,128)(2,1)S(1)}, u32[]{:S(2)}, u32[]{:S(2)}) collective-permute-start(bf16[592,384]{1,0:T(8,128)(2,1)S(1)} %fusion.10), channel_id=1, source_target_pairs={{0,2},{2,0},{4,6},{6,4},{1,3},{3,1},{5,7},{7,5},{8,10},{10,8},{12,... | collective-permute-start | bytes 1363976 | tf_op jit(solution)/shard_map/ppermute | solution.py:16
  116.3 21.8 %collective-permute-done.16 = bf16[592,384]{1,0:T(8,128)(2,1)} collective-permute-done((bf16[592,384]{1,0:T(8,128)(2,1)S(1)}, bf16[592,384]{1,0:T(8,128)(2,1)}, u32[]{:S(2)}, u32[]{:S(2)}) %collective-permute-start.16) | collective-permute-done | bytes 454688 | tf_op jit(solution)/shard_map/ppermute | solution.py:16
  138.1 3.9 %constant_dynamic-slice_fusion = (bf16[1,768,768]{2,1,0:T(8,128)(2,1)}, bf16[1,768,768]{2,1,0:T(8,128)(2,1)}, bf16[1,768,768]{2,1,0:T(8,128)(2,1)}) fusion(bf16[8,1536,768]{2,1,0:T(8,128)(2,1)} %tile_ref.11, s32[]{:T(128)S(6)} %select_n.61, s32[]{:T(128)S(6)} %select_n.60), kind=kLoop, calls=%fused_computation.92 | loop fusion | bytes 7077896 | tf_op jit(solution)/shard_map/dynamic_slice | solution.py:397
  143.4 1.5 collective-permute-start.19
  149.6 1.5 collective-permute-start.21
  151.1 2.8 pad_maximum_fusion
  153.9 2.9 collective-permute-done.19
  156.8 1.5 collective-permute-start.22
  160.9 5.7 %collective-permute-done.20 = bf16[592,384]{1,0:T(8,128)(2,1)} collective-permute-done((bf16[592,384]{1,0:T(8,128)(2,1)S(1)}, bf16[592,384]{1,0:T(8,128)(2,1)}, u32[]{:S(2)}, u32[]{:S(2)}) %collective-permute-start.20) | collective-permute-done | bytes 454688 | tf_op jit(solution)/shard_map/ppermute | solution.py:16
  168.4 7.9 %collective-permute-done.21 = bf16[592,384]{1,0:T(8,128)(2,1)} collective-permute-done((bf16[592,384]{1,0:T(8,128)(2,1)}, bf16[592,384]{1,0:T(8,128)(2,1)}, u32[]{:S(2)}, u32[]{:S(2)}) %collective-permute-start.21) | collective-permute-done | bytes 454688 | tf_op jit(solution)/shard_map/ppermute | solution.py:16
  176.9 5.2 %collective-permute-done.22 = bf16[592,384]{1,0:T(8,128)(2,1)} collective-permute-done((bf16[592,384]{1,0:T(8,128)(2,1)S(1)}, bf16[592,384]{1,0:T(8,128)(2,1)}, u32[]{:S(2)}, u32[]{:S(2)}) %collective-permute-start.22) | collective-permute-done | bytes 454688 | tf_op jit(solution)/shard_map/ppermute | solution.py:16
  182.6 3.1 pad_maximum_fusion.1
  185.7 1.5 collective-permute-start.29
  187.2 1.5 collective-permute-start.28
  188.7 13.8 %keep_tiles.1 = (bf16[1536,6144]{1,0:T(8,128)(2,1)}, bf16[6144,1536]{1,0:T(8,128)(2,1)}) custom-call(s32[3]{0:T(128)} %pad_add_fusion.place_ref, bf16[8,768,1536]{2,1,0:T(8,128)(2,1)} %tile_ref.7, bf16[8,1536,768]{2,1,0:T(8,128)(2,1)} %tile_ref.11), custom_call_target="tpu_custom_call" | custom-call | flops 5662310400 | bytes 37748736 | tf_op jit(solution)/shard_map/keep_tiles/pallas_call | solution.py:88
  203.6 2.1 copy.27
  205.7 2.4 pad_maximum_fusion.2.tokens_ref
  208.1 11.7 %layer_share.4 = (f32[1024,768]{1,0:T(8,128)}, bf16[1024,1536]{1,0:T(8,128)(2,1)}) custom-call(s32[2]{0:T(128)} %pad_add_fusion.2.place_ref, bf16[1024,592]{1,0:T(8,128)(2,1)} %pad_maximum_fusion.2.tokens_ref, f32[1024,1]{1,0:T(8,128)} %copy.28.scale_ref, f32[4,1,384]{2,1,0:T(1,128)} %get-tuple-element.69.bias_ref, bf16[8,1536,768]{2,1,0:T(8,128)(2,1)} %tile_ref.11, ...), custom_call_target="tpu_custom_call" | custom-call | flops 4278190080 | bytes 13615104 | tf_op jit(solution)/shard_map/layer_share/pallas_call | solution.py:283
  220.4 11.2 %collective-permute-done.29.refs_9_ = bf16[1,768,768]{2,1,0:T(8,128)(2,1)} collective-permute-done((bf16[1,768,768]{2,1,0:T(8,128)(2,1)}, bf16[1,768,768]{2,1,0:T(8,128)(2,1)}, u32[]{:S(2)}, u32[]{:S(2)}) %collective-permute-start.29) | collective-permute-done | bytes 1179680 | tf_op jit(solution)/shard_map/ppermute | solution.py:16
  232.2 12.1 %layer_share.5 = (f32[1024,768]{1,0:T(8,128)}, bf16[1024,1536]{1,0:T(8,128)(2,1)}) custom-call(s32[2]{0:T(128)} %pad_add_fusion.3.place_ref, bf16[1024,592]{1,0:T(8,128)(2,1)} %pad_maximum_fusion.2.tokens_ref, f32[1024,1]{1,0:T(8,128)} %copy.28.scale_ref, f32[4,1,384]{2,1,0:T(1,128)} %get-tuple-element.68.bias_ref, ...), custom_call_target="tpu_custom_call", output_to_operand_aliasing={{0}: (6, {})} | custom-call | flops 4278190080 | bytes 13615104 | tf_op jit(solution)/shard_map/layer_share/pallas_call | solution.py:283
  244.4 12.1 %layer_share.6 = (f32[1024,768]{1,0:T(8,128)}, bf16[1024,1536]{1,0:T(8,128)(2,1)}) custom-call(s32[2]{0:T(128)} %pad_add_fusion.4.place_ref, bf16[1024,592]{1,0:T(8,128)(2,1)} %pad_maximum_fusion.2.tokens_ref, f32[1024,1]{1,0:T(8,128)} %copy.28.scale_ref, f32[4,1,384]{2,1,0:T(1,128)} %get-tuple-element.67.bias_ref, ...), custom_call_target="tpu_custom_call", output_to_operand_aliasing={{0}: (9, {})} | custom-call | flops 4278190080 | bytes 13615104 | tf_op jit(solution)/shard_map/layer_share/pallas_call | solution.py:283
  256.5 1.6 collective-permute-start.2
  258.1 12.2 %layer_share.7 = (f32[1024,768]{1,0:T(8,128)}, bf16[1024,1536]{1,0:T(8,128)(2,1)}) custom-call(s32[2]{0:T(128)} %pad_add_fusion.5.place_ref, bf16[1024,592]{1,0:T(8,128)(2,1)} %pad_maximum_fusion.2.tokens_ref, f32[1024,1]{1,0:T(8,128)} %copy.28.scale_ref, f32[4,1,384]{2,1,0:T(1,128)} %get-tuple-element.66.bias_ref, ...), custom_call_target="tpu_custom_call", output_to_operand_aliasing={{0}: (6, {})} | custom-call | flops 4278190080 | bytes 13615104 | tf_op jit(solution)/shard_map/layer_share/pallas_call | solution.py:283
  271.3 11.6 %came_sum.2 = (bf16[512,768]{1,0:T(8,128)(2,1)}, bf16[6144,1536]{1,0:T(8,128)(2,1)}) custom-call(s32[3]{0:T(128)} %pad_add_fusion.place_ref, bf16[1024,1536]{1,0:T(8,128)(2,1)} %get-tuple-element.40.refs_0_, bf16[1024,1536]{1,0:T(8,128)(2,1)} %get-tuple-element.42.refs_1_, ...), custom_call_target="tpu_custom_call", output_to_operand_aliasing={{1}: (13, {})} | custom-call | flops 4831838208 | bytes 15728640 | tf_op jit(solution)/shard_map/came_sum/pallas_call | solution.py:242
  283.9 1.5 multiply_reduce_fusion.2
  288.3 11.7 %came_sum.3 = f32[512,768]{1,0:T(8,128)} custom-call(s32[3]{0:T(128)} %pad_add_fusion.place_ref, bf16[1024,1536]{1,0:T(8,128)(2,1)} %get-tuple-element.40.refs_0_, bf16[1024,1536]{1,0:T(8,128)(2,1)} %get-tuple-element.42.refs_1_, bf16[1024,1536]{1,0:T(8,128)(2,1)} %get-tuple-element.44.refs_2_, bf16[1024,1536]{1,0:T(8,128)(2,1)} %get-tuple-element.46.refs_3_, ...), custom_call_target="tpu_custom_call" | custom-call | flops 4831838208 | bytes 15728640 | tf_op jit(solution)/shard_map/came_sum/pallas_call | solution.py:242
  300.6 9.9 %collective-permute-done.6.refs_6_ = bf16[2,768,384]{2,1,0:T(8,128)(2,1)} collective-permute-done((bf16[2,768,384]{2,1,0:T(8,128)(2,1)}, bf16[2,768,384]{2,1,0:T(8,128)(2,1)}, u32[]{:S(2)}, u32[]{:S(2)}) %collective-permute-start.6) | collective-permute-done | bytes 1179680 | tf_op jit(solution)/shard_map/ppermute | solution.py:16
  311.0 1.6 convert_add_fusion.1
  312.6 7.2 %collective-permute-done.33 = bf16[512,768]{1,0:T(8,128)(2,1)} collective-permute-done((bf16[512,768]{1,0:T(8,128)(2,1)S(1)}, bf16[512,768]{1,0:T(8,128)(2,1)}, u32[]{:S(2)}, u32[]{:S(2)}) %collective-permute-start.33) | collective-permute-done | bytes 786464 | tf_op jit(solution)/shard_map/ppermute | solution.py:16
  321.8 1.8 fusion.14
  323.7 7.7 %collective-permute-done.34 = f32[528,128]{1,0:T(8,128)S(1)} collective-permute-done((f32[528,128]{1,0:T(8,128)S(1)}, f32[528,128]{1,0:T(8,128)S(1)}, u32[]{:S(2)}, u32[]{:S(2)}) %collective-permute-start.34) | collective-permute-done | bytes 270368 | tf_op jit(solution)/shard_map/ppermute | solution.py:16
  331.4 3.7 %collective-permute-start.35 = (f32[528,128]{1,0:T(8,128)S(1)}, f32[528,128]{1,0:T(8,128)S(1)}, u32[]{:S(2)}, u32[]{:S(2)}) collective-permute-start(f32[528,128]{1,0:T(8,128)S(1)} %fusion.47), channel_id=1, source_target_pairs={{0,4},{2,6},{4,0},{6,2},{1,5},{3,7},{5,1},{7,3},{8,12},{10,14},{12... | collective-permute-start | bytes 811016 | tf_op jit(solution)/shard_map/ppermute | solution.py:16
  336.1 8.2 %shard_map.130 = bf16[1536,6144]{1,0:T(8,128)(2,1)} custom-call(s32[3]{0:T(128)} %pad_add_fusion.place_ref, bf16[2,768,384]{2,1,0:T(8,128)(2,1)} %collective-permute-done.refs_0_, bf16[2,768,384]{2,1,0:T(8,128)(2,1)} %copy-done.11, bf16[2,768,384]{2,1,0:T(8,128)(2,1)} %collective-permute-done.2.refs_2_, ...), custom_call_target="tpu_custom_call", output_to_operand_aliasing={{}: (9, {})} | custom-call | flops 2831155200 | bytes 18874368 | tf_op jit(solution)/shard_map/pallas_call | solution.py:128
  344.3 1.9 collective-permute-done.35
  (138 shorter events, 37.1 us)
Async XLA Ops:
  0.6 115.6 %copy-start = (f32[48,6144]{1,0:T(8,128)S(1)}, f32[48,6144]{1,0:T(8,128)}, u32[]{:S(2)}) copy-start(f32[48,6144]{1,0:T(8,128)} %param.20) | copy-start | bytes 3538948
  1.3 4.1 %copy-start.17 = (f32[1536]{0:T(1024)S(1)}, f32[1536]{0:T(1024)}, u32[]{:S(2)}) copy-start(f32[1536]{0:T(1024)} %param.15) | copy-start | bytes 18436
  13.7 5.1 %collective-permute-start.8 = (f32[1613]{0:T(1024)S(1)}, f32[1613]{0:T(1024)S(1)}, u32[]{:S(2)}, u32[]{:S(2)}) collective-permute-start(f32[1613]{0:T(1024)S(1)} %concatenate.37), channel_id=1, source_target_pairs={{0,2},{2,0},{4,6},{6,4},{1,3},{3,1},{5,7},{7,5},{8,10},{10,8},{12,... | collective-permute-start | bytes 19364 | tf_op jit(solution)/shard_map/ppermute | solution.py:16
  16.7 29.2 %collective-permute-start = (bf16[2,768,384]{2,1,0:T(8,128)(2,1)}, bf16[2,768,384]{2,1,0:T(8,128)(2,1)}, u32[]{:S(2)}, u32[]{:S(2)}) collective-permute-start(bf16[2,768,384]{2,1,0:T(8,128)(2,1)} %get-tuple-element.30), channel_id=1, source_target_pairs={{0,1},{1,0},{2,3},{3,2},{4,5},{5,4},{6,7},{7,6},{8,9},{9,8},{10,11... | collective-permute-start | bytes 3538952 | tf_op jit(solution)/shard_map/ppermute | solution.py:16
  18.2 51.5 %collective-permute-start.4 = (bf16[2,768,384]{2,1,0:T(8,128)(2,1)}, bf16[2,768,384]{2,1,0:T(8,128)(2,1)}, u32[]{:S(2)}, u32[]{:S(2)}) collective-permute-start(bf16[2,768,384]{2,1,0:T(8,128)(2,1)} %get-tuple-element.31), channel_id=1, source_target_pairs={{0,1},{1,0},{2,3},{3,2},{4,5},{5,4},{6,7},{7,6},{8,9},{9,8},{10,11... | collective-permute-start | bytes 3538952 | tf_op jit(solution)/shard_map/ppermute | solution.py:16
  18.8 8.8 %collective-permute-start.9 = (f32[1613]{0:T(1024)S(1)}, f32[1613]{0:T(1024)S(1)}, u32[]{:S(2)}, u32[]{:S(2)}) collective-permute-start(f32[1613]{0:T(1024)S(1)} %add.155), channel_id=1, source_target_pairs={{0,4},{2,6},{4,0},{6,2},{1,5},{3,7},{5,1},{7,3},{8,12},{10,14},{12... | collective-permute-start | bytes 19364 | tf_op jit(solution)/shard_map/ppermute | solution.py:16
  47.6 29.1 %collective-permute-start.14 = (bf16[592,384]{1,0:T(8,128)(2,1)S(1)}, bf16[592,384]{1,0:T(8,128)(2,1)S(1)}, u32[]{:S(2)}, u32[]{:S(2)}) collective-permute-start(bf16[592,384]{1,0:T(8,128)(2,1)S(1)} %fusion.13), channel_id=1, source_target_pairs={{0,2},{2,0},{4,6},{6,4},{1,3},{3,1},{5,7},{7,5},{8,10},{10,8},{12,... | collective-permute-start | bytes 1363976 | tf_op jit(solution)/shard_map/ppermute | solution.py:16
  71.5 31.7 %collective-permute-start.13 = (bf16[592,384]{1,0:T(8,128)(2,1)S(1)}, bf16[592,384]{1,0:T(8,128)(2,1)S(1)}, u32[]{:S(2)}, u32[]{:S(2)}) collective-permute-start(bf16[592,384]{1,0:T(8,128)(2,1)S(1)} %fusion.12), channel_id=1, source_target_pairs={{0,4},{2,6},{4,0},{6,2},{1,5},{3,7},{5,1},{7,3},{8,12},{10,14},{12... | collective-permute-start | bytes 1363976 | tf_op jit(solution)/shard_map/ppermute | solution.py:16
  75.8 27.3 %collective-permute-start.12 = (bf16[592,384]{1,0:T(8,128)(2,1)S(1)}, bf16[592,384]{1,0:T(8,128)(2,1)S(1)}, u32[]{:S(2)}, u32[]{:S(2)}) collective-permute-start(bf16[592,384]{1,0:T(8,128)(2,1)S(1)} %fusion.11), channel_id=1, source_target_pairs={{0,6},{2,4},{4,2},{6,0},{1,7},{3,5},{5,3},{7,1},{8,14},{10,12},{12... | collective-permute-start | bytes 1363976 | tf_op jit(solution)/shard_map/ppermute | solution.py:16
  105.0 46.1 %copy-start.7 = (bf16[592,384]{1,0:T(8,128)(2,1)}, bf16[592,384]{1,0:T(8,128)(2,1)S(1)}, u32[]{:S(2)}) copy-start(bf16[592,384]{1,0:T(8,128)(2,1)S(1)} %fusion.10) | copy-start | bytes 1363972
  105.0 40.6 %collective-permute-start.15 = (bf16[592,384]{1,0:T(8,128)(2,1)S(1)}, bf16[592,384]{1,0:T(8,128)(2,1)S(1)}, u32[]{:S(2)}, u32[]{:S(2)}) collective-permute-start(bf16[592,384]{1,0:T(8,128)(2,1)S(1)} %fusion.10), channel_id=1, source_target_pairs={{0,2},{2,0},{4,6},{6,4},{1,3},{3,1},{5,7},{7,5},{8,10},{10,8},{12,... | collective-permute-start | bytes 1363976 | tf_op jit(solution)/shard_map/ppermute | solution.py:16
  115.2 22.9 %collective-permute-start.16 = (bf16[592,384]{1,0:T(8,128)(2,1)S(1)}, bf16[592,384]{1,0:T(8,128)(2,1)}, u32[]{:S(2)}, u32[]{:S(2)}) collective-permute-start(bf16[592,384]{1,0:T(8,128)(2,1)S(1)} %fusion.10), channel_id=1, source_target_pairs={{0,4},{2,6},{4,0},{6,2},{1,5},{3,7},{5,1},{7,3},{8,12},{10,14},{12... | collective-permute-start | bytes 1363976 | tf_op jit(solution)/shard_map/ppermute | solution.py:16
  138.1 13.0 %collective-permute-start.17 = (bf16[592,384]{1,0:T(8,128)(2,1)}, bf16[592,384]{1,0:T(8,128)(2,1)S(1)}, u32[]{:S(2)}, u32[]{:S(2)}) collective-permute-start(bf16[592,384]{1,0:T(8,128)(2,1)} %collective-permute-done.16), channel_id=1, source_target_pairs={{0,2},{2,0},{4,6},{6,4},{1,3},{3,1},{5,7},{7,5},{8,10},{10,8},{12,... | collective-permute-start | bytes 1363976 | tf_op jit(solution)/shard_map/ppermute | solution.py:16
  142.0 45.2 %collective-permute-start.24 = (bf16[1,768,768]{2,1,0:T(8,128)(2,1)}, bf16[1,768,768]{2,1,0:T(8,128)(2,1)S(1)}, u32[]{:S(2)}, u32[]{:S(2)}) collective-permute-start(bf16[1,768,768]{2,1,0:T(8,128)(2,1)} %get-tuple-element.64), channel_id=1, source_target_pairs={{0,1},{1,0},{2,3},{3,2},{4,5},{5,4},{6,7},{7,6},{8,9},{9,8},{10,11... | collective-permute-start | bytes 3538952 | tf_op jit(solution)/shard_map/ppermute | solution.py:16
  143.4 13.4 %collective-permute-start.19 = (bf16[592,384]{1,0:T(8,128)(2,1)S(1)}, bf16[592,384]{1,0:T(8,128)(2,1)}, u32[]{:S(2)}, u32[]{:S(2)}) collective-permute-start(bf16[592,384]{1,0:T(8,128)(2,1)S(1)} %fusion.10), channel_id=1, source_target_pairs={{0,16},{8,24},{16,0},{24,8},{1,17},{9,25},{17,1},{25,9},{2,18},{10... | collective-permute-start | bytes 1363976 | tf_op jit(solution)/shard_map/ppermute | solution.py:16
  145.6 8.3 %copy-start.8 = (bf16[592,384]{1,0:T(8,128)(2,1)}, bf16[592,384]{1,0:T(8,128)(2,1)S(1)}, u32[]{:S(2)}) copy-start(bf16[592,384]{1,0:T(8,128)(2,1)S(1)} %collective-permute-done.15) | copy-start | bytes 1363972
  145.6 21.0 %collective-permute-start.20 = (bf16[592,384]{1,0:T(8,128)(2,1)S(1)}, bf16[592,384]{1,0:T(8,128)(2,1)}, u32[]{:S(2)}, u32[]{:S(2)}) collective-permute-start(bf16[592,384]{1,0:T(8,128)(2,1)S(1)} %collective-permute-done.15), channel_id=1, source_target_pairs={{0,16},{8,24},{16,0},{24,8},{1,17},{9,25},{17,1},{25,9},{2,18},{10... | collective-permute-start | bytes 1363976 | tf_op jit(solution)/shard_map/ppermute | solution.py:16
  149.6 26.7 %collective-permute-start.21 = (bf16[592,384]{1,0:T(8,128)(2,1)}, bf16[592,384]{1,0:T(8,128)(2,1)}, u32[]{:S(2)}, u32[]{:S(2)}) collective-permute-start(bf16[592,384]{1,0:T(8,128)(2,1)} %collective-permute-done.16), channel_id=1, source_target_pairs={{0,16},{8,24},{16,0},{24,8},{1,17},{9,25},{17,1},{25,9},{2,18},{10... | collective-permute-start | bytes 1363976 | tf_op jit(solution)/shard_map/ppermute | solution.py:16
  151.1 5.7 %copy-start.9 = (bf16[592,384]{1,0:T(8,128)(2,1)}, bf16[592,384]{1,0:T(8,128)(2,1)S(1)}, u32[]{:S(2)}) copy-start(bf16[592,384]{1,0:T(8,128)(2,1)S(1)} %collective-permute-done.17) | copy-start | bytes 1363972
  153.9 78.3 %collective-permute-start.18 = (bf16[4,592,384]{2,1,0:T(8,128)(2,1)}, bf16[4,592,384]{2,1,0:T(8,128)(2,1)}, u32[]{:S(2)}, u32[]{:S(2)}) collective-permute-start(bf16[4,592,384]{2,1,0:T(8,128)(2,1)} %pad_maximum_fusion), channel_id=1, source_target_pairs={{0,8},{8,0},{16,24},{24,16},{1,9},{9,1},{17,25},{25,17},{2,10},{10... | collective-permute-start | bytes 5455880 | tf_op jit(solution)/shard_map/ppermute | solution.py:16
  156.8 25.2 %collective-permute-start.22 = (bf16[592,384]{1,0:T(8,128)(2,1)S(1)}, bf16[592,384]{1,0:T(8,128)(2,1)}, u32[]{:S(2)}, u32[]{:S(2)}) collective-permute-start(bf16[592,384]{1,0:T(8,128)(2,1)S(1)} %collective-permute-done.17), channel_id=1, source_target_pairs={{0,16},{8,24},{16,0},{24,8},{1,17},{9,25},{17,1},{25,9},{2,18},{10... | collective-permute-start | bytes 1363976 | tf_op jit(solution)/shard_map/ppermute | solution.py:16
  166.6 22.1 %collective-permute-start.10 = (bf16[512,592]{0,1:T(8,128)(2,1)}, bf16[512,592]{0,1:T(8,128)(2,1)}, u32[]{:S(2)}, u32[]{:S(2)}) collective-permute-start(bf16[512,592]{0,1:T(8,128)(2,1)} %copy.26), channel_id=1, source_target_pairs={{0,1},{1,0},{2,3},{3,2},{4,5},{5,4},{6,7},{7,6},{8,9},{9,8},{10,11... | collective-permute-start | bytes 1818632 | tf_op jit(solution)/shard_map/ppermute | solution.py:16
  176.3 9.3 %collective-permute-start.11 = (f32[512]{0:T(512)S(1)}, f32[512]{0:T(512)S(1)}, u32[]{:S(2)}, u32[]{:S(2)}) collective-permute-start(f32[512]{0:T(512)S(1)} %add_rsqrt_fusion), channel_id=1, source_target_pairs={{0,1},{1,0},{2,3},{3,2},{4,5},{5,4},{6,7},{7,6},{8,9},{9,8},{10,11... | collective-permute-start | bytes 6152 | tf_op jit(solution)/shard_map/ppermute | solution.py:16
  182.1 37.8 %collective-permute-start.25 = (bf16[1,768,768]{2,1,0:T(8,128)(2,1)}, bf16[1,768,768]{2,1,0:T(8,128)(2,1)S(1)}, u32[]{:S(2)}, u32[]{:S(2)}) collective-permute-start(bf16[1,768,768]{2,1,0:T(8,128)(2,1)} %get-tuple-element.65), channel_id=1, source_target_pairs={{0,1},{1,0},{2,3},{3,2},{4,5},{5,4},{6,7},{7,6},{8,9},{9,8},{10,11... | collective-permute-start | bytes 3538952 | tf_op jit(solution)/shard_map/ppermute | solution.py:16
  185.7 46.0 %collective-permute-start.29 = (bf16[1,768,768]{2,1,0:T(8,128)(2,1)}, bf16[1,768,768]{2,1,0:T(8,128)(2,1)}, u32[]{:S(2)}, u32[]{:S(2)}) collective-permute-start(bf16[1,768,768]{2,1,0:T(8,128)(2,1)} %get-tuple-element.63), channel_id=1, source_target_pairs={{0,1},{1,0},{2,3},{3,2},{4,5},{5,4},{6,7},{7,6},{8,9},{9,8},{10,11... | collective-permute-start | bytes 3538952 | tf_op jit(solution)/shard_map/ppermute | solution.py:16
  187.2 32.7 %copy-start.3 = (bf16[1,768,768]{2,1,0:T(8,128)(2,1)}, bf16[1,768,768]{2,1,0:T(8,128)(2,1)S(1)}, u32[]{:S(2)}) copy-start(bf16[1,768,768]{2,1,0:T(8,128)(2,1)S(1)} %collective-permute-done.24.refs_4_) | copy-start | bytes 3538948
  187.2 44.5 %collective-permute-start.28 = (bf16[1,768,768]{2,1,0:T(8,128)(2,1)S(1)}, bf16[1,768,768]{2,1,0:T(8,128)(2,1)}, u32[]{:S(2)}, u32[]{:S(2)}) collective-permute-start(bf16[1,768,768]{2,1,0:T(8,128)(2,1)S(1)} %collective-permute-done.24.refs_4_), channel_id=1, source_target_pairs={{0,16},{8,24},{16,0},{24,8},{1,17},{9,25},{17,1},{25,9},{2,18},{10... | collective-permute-start | bytes 3538952 | tf_op jit(solution)/shard_map/ppermute | solution.py:16
  188.7 67.8 %collective-permute-start.23 = (bf16[4,592,384]{2,1,0:T(8,128)(2,1)}, bf16[4,592,384]{2,1,0:T(8,128)(2,1)}, u32[]{:S(2)}, u32[]{:S(2)}) collective-permute-start(bf16[4,592,384]{2,1,0:T(8,128)(2,1)} %pad_maximum_fusion.1), channel_id=1, source_target_pairs={{0,8},{8,0},{16,24},{24,16},{1,9},{9,1},{17,25},{25,17},{2,10},{10... | collective-permute-start | bytes 5455880 | tf_op jit(solution)/shard_map/ppermute | solution.py:16
  219.9 24.5 %copy-start.4 = (bf16[1,768,768]{2,1,0:T(8,128)(2,1)}, bf16[1,768,768]{2,1,0:T(8,128)(2,1)S(1)}, u32[]{:S(2)}) copy-start(bf16[1,768,768]{2,1,0:T(8,128)(2,1)S(1)} %collective-permute-done.25.refs_5_) | copy-start | bytes 3538948
  219.9 50.4 %collective-permute-start.26 = (bf16[1,768,768]{2,1,0:T(8,128)(2,1)S(1)}, bf16[1,768,768]{2,1,0:T(8,128)(2,1)S(1)}, u32[]{:S(2)}, u32[]{:S(2)}) collective-permute-start(bf16[1,768,768]{2,1,0:T(8,128)(2,1)S(1)} %collective-permute-done.24.refs_4_), channel_id=1, source_target_pairs={{0,8},{8,0},{16,24},{24,16},{1,9},{9,1},{17,25},{25,17},{2,10},{10... | collective-permute-start | bytes 3538952 | tf_op jit(solution)/shard_map/ppermute | solution.py:16
  231.7 39.2 %collective-permute-start.27 = (bf16[1,768,768]{2,1,0:T(8,128)(2,1)S(1)}, bf16[1,768,768]{2,1,0:T(8,128)(2,1)}, u32[]{:S(2)}, u32[]{:S(2)}) collective-permute-start(bf16[1,768,768]{2,1,0:T(8,128)(2,1)S(1)} %collective-permute-done.25.refs_5_), channel_id=1, source_target_pairs={{0,8},{8,0},{16,24},{24,16},{1,9},{9,1},{17,25},{25,17},{2,10},{10... | collective-permute-start | bytes 3538952 | tf_op jit(solution)/shard_map/ppermute | solution.py:16
  231.7 39.2 %collective-permute-start.31 = (bf16[1,768,768]{2,1,0:T(8,128)(2,1)}, bf16[1,768,768]{2,1,0:T(8,128)(2,1)}, u32[]{:S(2)}, u32[]{:S(2)}) collective-permute-start(bf16[1,768,768]{2,1,0:T(8,128)(2,1)} %collective-permute-done.29.refs_9_), channel_id=1, source_target_pairs={{0,8},{8,0},{16,24},{24,16},{1,9},{9,1},{17,25},{25,17},{2,10},{10... | collective-permute-start | bytes 3538952 | tf_op jit(solution)/shard_map/ppermute | solution.py:16
  232.2 38.7 %collective-permute-start.30 = (bf16[1,768,768]{2,1,0:T(8,128)(2,1)}, bf16[1,768,768]{2,1,0:T(8,128)(2,1)}, u32[]{:S(2)}, u32[]{:S(2)}) collective-permute-start(bf16[1,768,768]{2,1,0:T(8,128)(2,1)} %collective-permute-done.28.refs_8_), channel_id=1, source_target_pairs={{0,8},{8,0},{16,24},{24,16},{1,9},{9,1},{17,25},{25,17},{2,10},{10... | collective-permute-start | bytes 3538952 | tf_op jit(solution)/shard_map/ppermute | solution.py:16
  256.5 43.5 %collective-permute-start.2 = (bf16[2,768,384]{2,1,0:T(8,128)(2,1)}, bf16[2,768,384]{2,1,0:T(8,128)(2,1)}, u32[]{:S(2)}, u32[]{:S(2)}) collective-permute-start(bf16[2,768,384]{2,1,0:T(8,128)(2,1)} %collective-permute-done.refs_0_), channel_id=1, source_target_pairs={{0,16},{8,24},{16,0},{24,8},{1,17},{9,25},{17,1},{25,9},{2,18},{10... | collective-permute-start | bytes 3538952 | tf_op jit(solution)/shard_map/ppermute | solution.py:16
  270.3 40.2 %collective-permute-start.6 = (bf16[2,768,384]{2,1,0:T(8,128)(2,1)}, bf16[2,768,384]{2,1,0:T(8,128)(2,1)}, u32[]{:S(2)}, u32[]{:S(2)}) collective-permute-start(bf16[2,768,384]{2,1,0:T(8,128)(2,1)} %collective-permute-done.4.refs_4_), channel_id=1, source_target_pairs={{0,16},{8,24},{16,0},{24,8},{1,17},{9,25},{17,1},{25,9},{2,18},{10... | collective-permute-start | bytes 3538952 | tf_op jit(solution)/shard_map/ppermute | solution.py:16
  271.3 12.5 %copy-start.18 = (f32[1536]{0:T(1024)S(1)}, f32[1536]{0:T(1024)}, u32[]{:S(2)}) copy-start(f32[1536]{0:T(1024)} %param.22) | copy-start | bytes 18436
  271.3 12.5 %copy-start.10 = (bf16[1536,128]{1,0:T(8,128)(2,1)S(1)}, bf16[1536,128]{1,0:T(8,128)(2,1)}, u32[]{:S(2)}) copy-start(bf16[1536,128]{1,0:T(8,128)(2,1)} %param.23) | copy-start | bytes 1179652
  282.9 27.6 %collective-permute-start.32 = (bf16[512,768]{1,0:T(8,128)(2,1)}, bf16[512,768]{1,0:T(8,128)(2,1)S(1)}, u32[]{:S(2)}, u32[]{:S(2)}) collective-permute-start(bf16[512,768]{1,0:T(8,128)(2,1)} %get-tuple-element.51), channel_id=1, source_target_pairs={{0,1},{1,0},{2,3},{3,2},{4,5},{5,4},{6,7},{7,6},{8,9},{9,8},{10,11... | collective-permute-start | bytes 2359304 | tf_op jit(solution)/shard_map/ppermute | solution.py:16
  286.9 32.9 %collective-permute-start.33 = (bf16[512,768]{1,0:T(8,128)(2,1)S(1)}, bf16[512,768]{1,0:T(8,128)(2,1)}, u32[]{:S(2)}, u32[]{:S(2)}) collective-permute-start(bf16[512,768]{1,0:T(8,128)(2,1)S(1)} %slice.170), channel_id=1, source_target_pairs={{0,1},{1,0},{2,3},{3,2},{4,5},{5,4},{6,7},{7,6},{8,9},{9,8},{10,11... | collective-permute-start | bytes 2359304 | tf_op jit(solution)/shard_map/ppermute | solution.py:16
  288.2 46.8 %collective-permute-start.1 = (bf16[2,768,384]{2,1,0:T(8,128)(2,1)}, bf16[2,768,384]{2,1,0:T(8,128)(2,1)S(1)}, u32[]{:S(2)}, u32[]{:S(2)}) collective-permute-start(bf16[2,768,384]{2,1,0:T(8,128)(2,1)} %collective-permute-done.refs_0_), channel_id=1, source_target_pairs={{0,8},{8,0},{16,24},{24,16},{1,9},{9,1},{17,25},{25,17},{2,10},{10... | collective-permute-start | bytes 3538952 | tf_op jit(solution)/shard_map/ppermute | solution.py:16
  300.0 19.8 %copy-start.2 = (f32[512,768]{1,0:T(8,128)S(1)}, f32[512,768]{1,0:T(8,128)}, u32[]{:S(2)}) copy-start(f32[512,768]{1,0:T(8,128)} %came_sum.3) | copy-start | bytes 4718596
  300.0 35.0 %collective-permute-start.5 = (bf16[2,768,384]{2,1,0:T(8,128)(2,1)}, bf16[2,768,384]{2,1,0:T(8,128)(2,1)}, u32[]{:S(2)}, u32[]{:S(2)}) collective-permute-start(bf16[2,768,384]{2,1,0:T(8,128)(2,1)} %collective-permute-done.4.refs_4_), channel_id=1, source_target_pairs={{0,8},{8,0},{16,24},{24,16},{1,9},{9,1},{17,25},{25,17},{2,10},{10... | collective-permute-start | bytes 3538952 | tf_op jit(solution)/shard_map/ppermute | solution.py:16
  310.5 24.6 %collective-permute-start.3 = (bf16[2,768,384]{2,1,0:T(8,128)(2,1)}, bf16[2,768,384]{2,1,0:T(8,128)(2,1)}, u32[]{:S(2)}, u32[]{:S(2)}) collective-permute-start(bf16[2,768,384]{2,1,0:T(8,128)(2,1)} %collective-permute-done.2.refs_2_), channel_id=1, source_target_pairs={{0,8},{8,0},{16,24},{24,16},{1,9},{9,1},{17,25},{25,17},{2,10},{10... | collective-permute-start | bytes 3538952 | tf_op jit(solution)/shard_map/ppermute | solution.py:16
  310.5 24.6 %collective-permute-start.7 = (bf16[2,768,384]{2,1,0:T(8,128)(2,1)}, bf16[2,768,384]{2,1,0:T(8,128)(2,1)}, u32[]{:S(2)}, u32[]{:S(2)}) collective-permute-start(bf16[2,768,384]{2,1,0:T(8,128)(2,1)} %collective-permute-done.6.refs_6_), channel_id=1, source_target_pairs={{0,8},{8,0},{16,24},{24,16},{1,9},{9,1},{17,25},{25,17},{2,10},{10... | collective-permute-start | bytes 3538952 | tf_op jit(solution)/shard_map/ppermute | solution.py:16
  312.6 8.5 %copy-start.6 = (f32[512,1536]{1,0:T(8,128)S(1)}, f32[512,1536]{1,0:T(8,128)}, u32[]{:S(2)}) copy-start(f32[512,1536]{1,0:T(8,128)} %get-tuple-element.70) | copy-start | bytes 9437188
  323.6 7.8 %collective-permute-start.34 = (f32[528,128]{1,0:T(8,128)S(1)}, f32[528,128]{1,0:T(8,128)S(1)}, u32[]{:S(2)}, u32[]{:S(2)}) collective-permute-start(f32[528,128]{1,0:T(8,128)S(1)} %pad_maximum_fusion.4), channel_id=1, source_target_pairs={{0,2},{2,0},{4,6},{6,4},{1,3},{3,1},{5,7},{7,5},{8,10},{10,8},{12,... | collective-permute-start | bytes 811016 | tf_op jit(solution)/shard_map/ppermute | solution.py:16
  331.4 14.8 %collective-permute-start.35 = (f32[528,128]{1,0:T(8,128)S(1)}, f32[528,128]{1,0:T(8,128)S(1)}, u32[]{:S(2)}, u32[]{:S(2)}) collective-permute-start(f32[528,128]{1,0:T(8,128)S(1)} %fusion.47), channel_id=1, source_target_pairs={{0,4},{2,6},{4,0},{6,2},{1,5},{3,7},{5,1},{7,3},{8,12},{10,14},{12... | collective-permute-start | bytes 811016 | tf_op jit(solution)/shard_map/ppermute | solution.py:16
  336.1 11.1 %copy-start.1 = (f32[48,6144]{1,0:T(8,128)S(1)}, f32[48,6144]{1,0:T(8,128)}, u32[]{:S(2)}) copy-start(f32[48,6144]{1,0:T(8,128)} %param.20) | copy-start | bytes 3538948
  (9 other events, 16.0 us)

commit v2 on v1

--- a/solution.py
+++ b/solution.py
@@ -175,25 +175,35 @@
     return [parts[k] for k in sorted(parts)]
 
 
+CHUNK = 2
+
+
 def layer_body(place_ref, tokens_ref, scale_ref, bias_ref, tile_ref, *refs, groups, adds):
     pieces = [ref.at[i] for ref in refs[:groups] for i in range(ref.shape[0])]
-    sum_ref, hidden_ref = refs[-2:]
+    sum_ref, hidden_ref, weight = refs[-3:]
     row, width = place_ref[1], pieces[0].shape[-1]
-    tokens = tokens_ref[...]
+
+    @pl.when(pl.program_id(0) == 0)
+    def _():
+        for j, piece in enumerate(pieces):
+            weight[:, pl.ds(pl.multiple_of((row ^ j) * width, width), width)] = piece[...]
+
+    tokens, scale = tokens_ref[...], scale_ref[...]
     total = refs[groups][...] if adds else None
-    for j, piece in enumerate(pieces):
-        start = pl.multiple_of((row ^ j) * width, width)
-        pre = jnp.dot(tokens, piece[...], preferred_element_type=jnp.float32)
-        pre = pre * scale_ref[...] + bias_ref[row ^ j]
+    size = weight.shape[1] // CHUNK
+    for n in range(CHUNK):
+        columns = pl.ds(n * size, size)
+        pre = jnp.dot(tokens, weight[:, columns], preferred_element_type=jnp.float32)
+        pre = pre * scale + bias_ref[:, columns]
         half = 0.5 * pre
         hidden = (half + half * lax.erf(pre * (0.5**0.5))).astype(jnp.bfloat16)
-        hidden_ref[:, pl.ds(start, width)] = hidden
-        term = jnp.dot(hidden, tile_ref[0, pl.ds(start, width), :], preferred_element_type=jnp.float32)
+        hidden_ref[:, columns] = hidden
+        term = jnp.dot(hidden, tile_ref[0, columns, :], preferred_element_type=jnp.float32)
         total = term if total is None else total + term
-    sum_ref[...] = total
-
-
-def came_body(place_ref, *refs, first, shares, halves, fills):
+    sum_ref[...] = total.astype(sum_ref.dtype)
+
+
+def came_body(place_ref, *refs, firsts, shares, halves, fills):
     value_refs, part_refs = refs[:shares], refs[shares : shares * (1 + halves)]
     refs = refs[shares * (1 + halves) + fills :]
     sum_ref, refs = refs[0], refs[1:]
@@ -204,7 +214,7 @@
     height, features = parts.shape[1] // halves, parts.shape[2]
     reads = []
     for k in range(shares):
-        group = [pltpu.make_async_copy(value_refs[k].at[pl.ds(first, count)], values.at[k], arrive.at[k, 0])]
+        group = [pltpu.make_async_copy(value_refs[k].at[pl.ds(firsts[k], count)], values.at[k], arrive.at[k, 0])]
         for h in range(halves):
             group.append(
                 pltpu.make_async_copy(
@@ -233,14 +243,15 @@
         copy.wait()
 
 
-def came_sum(place, values, parts, first, count, kind, weight):
+def came_sum(place, values, parts, count, kind, weight):
+    values, firsts = zip(*values)
     shares, halves = len(values), len(parts) // len(values)
     width, features = values[0].shape[1], parts[0].shape[2]
     hbm = pl.BlockSpec(memory_space=pl.ANY)
     fills = weight is not None
     outs = [jax.ShapeDtypeStruct((count, features), kind)]
     return pl.pallas_call(
-        functools.partial(came_body, first=first, shares=shares, halves=halves, fills=int(fills)),
+        functools.partial(came_body, firsts=firsts, shares=shares, halves=halves, fills=int(fills)),
         in_specs=[pl.BlockSpec(memory_space=pltpu.SMEM)] + [hbm] * (len(values) + len(parts) + fills),
         out_specs=[pl.BlockSpec(memory_space=pltpu.VMEM)] + [hbm] * fills,
         out_shape=outs + ([jax.ShapeDtypeStruct(weight.shape, weight.dtype)] if fills else []),
@@ -261,33 +272,36 @@
     )(place, *values, *parts, *((weight,) if fills else ()))
 
 
-def layer_share(place, tokens, scale, bias, tiles, pieces, total, block):
-    count, depth = tokens.shape
+def layer_share(place, tokens, scale, bias, tiles, pieces, total, block, first, count, kind):
+    depth = tokens.shape[1]
     _, tile_rows, tile_cols = tiles.shape
+    skip = first // block
+    same = total is not None and total.shape[0] == count
     spec = pltpu.PrefetchScalarGridSpec(
         num_scalar_prefetch=1,
         grid=(count // block,),
         in_specs=[
-            pl.BlockSpec((block, depth), lambda i, s: (i, 0)),
-            pl.BlockSpec((block, 1), lambda i, s: (i, 0)),
-            pl.BlockSpec(bias.shape, lambda i, s: (0, 0, 0)),
+            pl.BlockSpec((block, depth), lambda i, s: (i + skip, 0)),
+            pl.BlockSpec((block, 1), lambda i, s: (i + skip, 0)),
+            pl.BlockSpec(bias.shape, lambda i, s: (0, 0)),
             pl.BlockSpec((1, tile_rows, tile_cols), lambda i, s: (s[0], 0, 0)),
         ]
         + [pl.BlockSpec(piece.shape, lambda i, s: (0, 0, 0)) for piece in pieces]
-        + ([] if total is None else [pl.BlockSpec((block, tile_cols), lambda i, s: (i, 0))]),
+        + ([] if total is None else [pl.BlockSpec((block, tile_cols), lambda i, s: (i + skip, 0))]),
         out_specs=[
             pl.BlockSpec((block, tile_cols), lambda i, s: (i, 0)),
             pl.BlockSpec((block, tile_rows), lambda i, s: (i, 0)),
         ],
+        scratch_shapes=[pltpu.VMEM((depth, tile_rows), tokens.dtype)],
     )
     return pl.pallas_call(
         functools.partial(layer_body, groups=len(pieces), adds=total is not None),
         grid_spec=spec,
         out_shape=[
-            jax.ShapeDtypeStruct((count, tile_cols), jnp.float32),
+            jax.ShapeDtypeStruct((count, tile_cols), kind),
             jax.ShapeDtypeStruct((count, tile_rows), jnp.bfloat16),
         ],
-        input_output_aliases={} if total is None else {5 + len(pieces): 0},
+        input_output_aliases={5 + len(pieces): 0} if same else {},
         cost_estimate=pl.CostEstimate(
             flops=2 * count * tile_rows * (depth + tile_cols),
             transcendentals=count * tile_rows,
@@ -385,20 +399,6 @@
         ),
         "row",
     ) / feature_count
-    one, late, sums = lax.optimization_barrier((jnp.ones((tokens, 1), patches.dtype), (1 - col) * (tiles_here // 2), sums))
-    tokens_in = jnp.concatenate(
-        [patches, one, jnp.zeros((tokens, depth - patch - 1), patches.dtype)], axis=1
-    )
-    tokens_in = gather_xor(tokens_in, "col")
-    if pair:
-        height = tile_cols // 2
-
-        def out_half(k, half):
-            sent = lax.dynamic_slice(old_out, (late + (rep ^ k), half * height, 0), (1, height, tile_rows))
-            return swap(sent, "col", 1)
-
-        out_parts = {(0, 0): out_half(0, 0), (0, 1): out_half(0, 1), (2, 1): out_half(2, 1)}
-
     average, square = sums[:tokens], sums[tokens : 2 * tokens]
     scale = gather_xor(lax.rsqrt(square - average * average + EPSILON), "col")[:, None]
 
@@ -423,7 +423,23 @@
         m, i = (0, k) if k < cut[0] else (1, k - cut[0])
         return times(centered[:, :tile_rows], in_mine[m][i]) + times(centered[:, tile_rows:], in_came[m][i])
 
-    came = [swap(partial(k).astype(jnp.bfloat16), "row", k) for k in reversed(range(1, rows))]
+    first_sent = partial(rows - 1).astype(jnp.bfloat16)
+    one, late, first_sent = lax.optimization_barrier((jnp.ones((tokens, 1), patches.dtype), (1 - col) * (tiles_here // 2), first_sent))
+    tokens_in = jnp.concatenate(
+        [patches, one, jnp.zeros((tokens, depth - patch - 1), patches.dtype)], axis=1
+    )
+    tokens_in = gather_xor(tokens_in, "col")
+    if pair:
+        height = tile_cols // 2
+
+        def out_half(k, half):
+            sent = lax.dynamic_slice(old_out, (late + (rep ^ k), half * height, 0), (1, height, tile_rows))
+            return swap(sent, "col", 1)
+
+        out_parts = {(0, 0): out_half(0, 0), (0, 1): out_half(0, 1), (2, 1): out_half(2, 1)}
+
+    came = [swap(first_sent, "row", rows - 1)]
+    came += [swap(partial(k).astype(jnp.bfloat16), "row", k) for k in reversed(range(1, rows - 1))]
     folded = partial(0)
     for value in came:
         folded = folded + value.astype(jnp.float32)
@@ -437,7 +453,8 @@
                 if mask > 1:
                     groups[k ^ mask] = [swap(value, "rep", mask) for value in groups[k]]
                 else:
-                    groups[k ^ mask] = [swap(jnp.stack(groups[k]), "rep", mask)]
+                    joined = jnp.stack(groups[k])
+                    groups[k ^ mask] = [swap(joined, "rep", mask)]
         in_parts = [spread(part, "rep") for part in in_came]
         out_parts[2, 0] = swap(out_parts[0, 0], "rep", 2)
         for k, half in sorted(out_parts):
@@ -449,25 +466,30 @@
             functools.partial(fill_in_body, parts=reps, counts=cut, rows=rows),
             reps * rows,
         )
-        biases = in_bias.reshape(reps, rows, 1, piece)
-        branch_mine = None
+        biases = in_bias.reshape(reps, 1, share)
         order = sorted(groups, key=lambda k: (bin(k).count("1"), k))
-        values = {}
-        for k in order:
+        block = min(256, tokens)
+
+        def layer(k, total, first, count, kind):
             pieces = [value if value.ndim == 3 else value[None] for value in groups[k]]
             place = jnp.stack([own + (rep ^ k), row]).astype(jnp.int32)
             bias = lax.dynamic_index_in_dim(biases, rep ^ k, 0, keepdims=False)
-            branch_mine, values[k] = layer_share(
-                place, tokens_in, scale, bias, old_out, pieces, branch_mine, min(256, tokens_in.shape[0])
-            )
-
-        shares = [values[k] for k in sorted(values)]
+            return layer_share(place, tokens_in, scale, bias, old_out, pieces, total, block, first, count, kind)
+
+        branch_mine, values = None, {}
+        for k in order[:-1]:
+            branch_mine, values[k] = layer(k, branch_mine, 0, 2 * tokens, jnp.float32)
+        last = order[-1]
+        theirs, value_theirs = layer(last, branch_mine, tokens, tokens, jnp.bfloat16)
+        to_came = swap(theirs, "col", 1).astype(jnp.float32)
+        branch_mine, value_ours = layer(last, branch_mine, 0, tokens, jnp.float32)
         parts = [out_parts[key] for key in sorted(out_parts)]
-        to_came = swap(branch_mine[tokens:].astype(jnp.bfloat16), "col", 1).astype(jnp.float32)
-        theirs, out_weight = came_sum(where, shares, parts, tokens, tokens, jnp.bfloat16, out_weight)
+        shares = [(values[k], tokens) for k in sorted(values)] + [(value_theirs, 0)]
+        theirs, out_weight = came_sum(where, shares, parts, tokens, jnp.bfloat16, out_weight)
         to_mine = swap(theirs, "col", 1).astype(jnp.float32)
-        (branch_came,) = came_sum(where, shares, parts, 0, tokens, jnp.float32, None)
-        branch = jnp.concatenate([branch_mine[:tokens] + to_mine, branch_came + to_came], axis=1)
+        shares = [(values[k], 0) for k in sorted(values)] + [(value_ours, 0)]
+        (branch_came,) = came_sum(where, shares, parts, tokens, jnp.float32, None)
+        branch = jnp.concatenate([branch_mine + to_mine, branch_came + to_came], axis=1)
     else:
         group = jnp.take(jnp.stack(group), row ^ jnp.arange(rows), axis=0)
         shares = jnp.take(jnp.stack(spread(group, "rep")), rep ^ jnp.arange(reps), axis=0)

time: 348 us -> 332 us (0.954)
  waiting for transfers between devices: 143 us -> 133 us
  starting transfers between devices: 43.5 us -> 35.9 us
  matrix products: 14.5 us -> 19.7 us
    ppermute x36, waiting for transfers between devices: 143 us -> 133 us  [swap(): return lax.ppermute(value, axis, pairs)]
    ppermute x36, starting transfers between devices: 43.5 us -> 35.9 us  [swap(): return lax.ppermute(value, axis, pairs)]
    dot_general x9, matrix products: 11.3 us -> 16.5 us  [times(): return jnp.dot(left, right, preferred_element_type=jnp.float32)]
    pallas_call x4 -> x5, Pallas kernels: 48.2 us -> 47.9 us  [layer_share(): pl.pallas_call(functools.partial(layer_body, groups=len(pieces), adds=tot...]
  transfers between devices with their start and end apart: 36 -> 36, of which waited for: 13 -> 15; matrix products, arithmetic and copies ran while one was open for 12% -> 13% of each run, Pallas kernels for 28% -> 29%
where the time goes in v2:
time: 332 us; the launch traced here: 331 us
  waiting for transfers between devices  133 us (40%)
  Pallas kernels  101 us (30%)
  starting transfers between devices  35.9 us (11%)
  other arithmetic  22.1 us (7%)
  matrix products  19.7 us (6%)
  local copies, waits for them, and re-layouts  17.1 us (5%)
    ppermute x36, waiting for transfers between devices, swap(): return lax.ppermute(value, axis, pairs)  133 us
    pallas_call x5, Pallas kernels, layer_share(): pl.pallas_call(functools.partial(layer_body, groups=len(pieces), adds=tot...  47.9 us
    ppermute x36, starting transfers between devices, swap(): return lax.ppermute(value, axis, pairs)  35.9 us
    pallas_call x2, Pallas kernels, came_sum(): pl.pallas_call(functools.partial(came_body, firsts=firsts, shares=shares,...  23.5 us
    dot_general x9, matrix products, times(): return jnp.dot(left, right, preferred_element_type=jnp.float32)  16.5 us
    pallas_call x1, Pallas kernels, keep_tiles(): pl.pallas_call(functools.partial(keep_body, kept=kept), in_specs=[pl.Bloc...  13.8 us
    pallas_call x1, Pallas kernels, fill(): pl.pallas_call(body, in_specs=[pl.BlockSpec(memory_space=pltpu.SMEM)] + [...  8.21 us
    pallas_call x2, Pallas kernels, cut_tile(): pl.pallas_call(cut_body, grid_spec=spec, out_shape=[jax.ShapeDtypeStruct(...  7.91 us
  transfers between devices with their start and end apart: 36, of which 15 were waited for; matrix products, arithmetic and copies ran while one was open for 13% of the time, Pallas kernels for 29%

profile of v2, /device:TPU:0, one launch (start us, length us, event | category | flops | bytes accessed | tf_op | source)
XLA Modules:
  0.0 330.6 jit_solution(4946231069611445395)
XLA Ops:
  1.2 3.9 %cut_tile.2 = (bf16[2,768,384]{2,1,0:T(8,128)(2,1)}, bf16[2,768,384]{2,1,0:T(8,128)(2,1)}) custom-call(s32[2]{0:T(128)} %pad_add_fusion.1.place_ref, bf16[8,768,1536]{2,1,0:T(8,128)(2,1)} %tile_ref.8), custom_call_target="tpu_custom_call" | custom-call | tf_op jit(solution)/shard_map/cut_tile/pallas_call | solution.py:162
  5.2 3.6 %convert_reduce_fusion = (f32[588]{0:T(1024)S(1)}, bf16[588,1536]{1,0:T(8,128)(2,1)S(1)}) fusion(s32[]{:T(128)S(6)} %select_n.55, bf16[588,1536]{1,0:T(8,128)(2,1)} %param.14), kind=kLoop, calls=%fused_computation.1 | loop fusion | flops 5418420 | bytes 3615028 | tf_op jit(solution)/shard_map/reduce_sum | solution.py:396
  9.5 3.2 multiply_reduce_fusion.1
  13.5 3.1 collective-permute-start.8
  18.6 2.6 collective-permute-start.9
  22.5 4.0 %cut_tile.3 = (bf16[2,768,384]{2,1,0:T(8,128)(2,1)}, bf16[2,768,384]{2,1,0:T(8,128)(2,1)}) custom-call(s32[2]{0:T(128)} %pad_add_fusion.2.place_ref, bf16[8,768,1536]{2,1,0:T(8,128)(2,1)} %tile_ref.8), custom_call_target="tpu_custom_call" | custom-call | tf_op jit(solution)/shard_map/cut_tile/pallas_call | solution.py:162
  33.0 12.6 %collective-permute-done.4.refs_4_ = bf16[2,768,384]{2,1,0:T(8,128)(2,1)} collective-permute-done((bf16[2,768,384]{2,1,0:T(8,128)(2,1)}, bf16[2,768,384]{2,1,0:T(8,128)(2,1)}, u32[]{:S(2)}, u32[]{:S(2)}) %collective-permute-start.4) | collective-permute-done | bytes 1179680 | tf_op jit(solution)/shard_map/ppermute | solution.py:16
  45.7 2.5 fusion.12
  48.2 2.6 collective-permute-start.13
  50.8 18.8 %collective-permute-done.refs_0_ = bf16[2,768,384]{2,1,0:T(8,128)(2,1)} collective-permute-done((bf16[2,768,384]{2,1,0:T(8,128)(2,1)}, bf16[2,768,384]{2,1,0:T(8,128)(2,1)}, u32[]{:S(2)}, u32[]{:S(2)}) %collective-permute-start) | collective-permute-done | bytes 1179680 | tf_op jit(solution)/shard_map/ppermute | solution.py:16
  69.6 2.5 fusion.13
  72.4 2.5 fusion.11
  74.9 3.7 %collective-permute-start.12 = (bf16[592,384]{1,0:T(8,128)(2,1)}, bf16[592,384]{1,0:T(8,128)(2,1)}, u32[]{:S(2)}, u32[]{:S(2)}) collective-permute-start(bf16[592,384]{1,0:T(8,128)(2,1)} %fusion.11), channel_id=1, source_target_pairs={{0,6},{2,4},{4,2},{6,0},{1,7},{3,5},{5,3},{7,1},{8,14},{10,12},{12... | collective-permute-start | bytes 1363976 | tf_op jit(solution)/shard_map/ppermute | solution.py:16
  78.6 2.6 fusion.19
  81.2 2.4 collective-permute-done.14
  83.6 11.6 %collective-permute-done.12 = bf16[592,384]{1,0:T(8,128)(2,1)} collective-permute-done((bf16[592,384]{1,0:T(8,128)(2,1)}, bf16[592,384]{1,0:T(8,128)(2,1)}, u32[]{:S(2)}, u32[]{:S(2)}) %collective-permute-start.12) | collective-permute-done | bytes 454688 | tf_op jit(solution)/shard_map/ppermute | solution.py:16
  95.2 2.7 fusion.10
  98.0 3.2 collective-permute-start.16
  101.2 3.8 %constant_dynamic-slice_fusion = (bf16[1,768,768]{2,1,0:T(8,128)(2,1)}, bf16[1,768,768]{2,1,0:T(8,128)(2,1)}, bf16[1,768,768]{2,1,0:T(8,128)(2,1)}) fusion(bf16[8,1536,768]{2,1,0:T(8,128)(2,1)} %tile_ref.13, s32[]{:T(128)S(6)} %select_n.62, s32[]{:T(128)S(6)} %select_n.61), kind=kLoop, calls=%fused_computation.92 | loop fusion | bytes 7077896 | tf_op jit(solution)/shard_map/dynamic_slice | solution.py:436
  106.5 12.6 %collective-permute-done.16 = bf16[592,384]{1,0:T(8,128)(2,1)S(1)} collective-permute-done((bf16[592,384]{1,0:T(8,128)(2,1)S(1)}, bf16[592,384]{1,0:T(8,128)(2,1)S(1)}, u32[]{:S(2)}, u32[]{:S(2)}) %collective-permute-start.16) | collective-permute-done | bytes 454688 | tf_op jit(solution)/shard_map/ppermute | solution.py:16
  119.2 1.5 copy.25
  121.4 1.5 collective-permute-start.19
  124.4 2.9 collective-permute-done.15
  127.3 7.9 %collective-permute-done.17 = bf16[592,384]{1,0:T(8,128)(2,1)} collective-permute-done((bf16[592,384]{1,0:T(8,128)(2,1)S(1)}, bf16[592,384]{1,0:T(8,128)(2,1)}, u32[]{:S(2)}, u32[]{:S(2)}) %collective-permute-start.17) | collective-permute-done | bytes 454688 | tf_op jit(solution)/shard_map/ppermute | solution.py:16
  135.2 2.6 pad_maximum_fusion
  140.9 1.5 collective-permute-start.20
  142.9 1.5 collective-permute-start.22
  144.5 13.8 %keep_tiles.1 = (bf16[1536,6144]{1,0:T(8,128)(2,1)}, bf16[6144,1536]{1,0:T(8,128)(2,1)}) custom-call(s32[3]{0:T(128)} %pad_add_fusion.place_ref, bf16[8,768,1536]{2,1,0:T(8,128)(2,1)} %tile_ref.8, bf16[8,1536,768]{2,1,0:T(8,128)(2,1)} %tile_ref.13), custom_call_target="tpu_custom_call" | custom-call | flops 5662310400 | bytes 37748736 | tf_op jit(solution)/shard_map/keep_tiles/pallas_call | solution.py:88
  160.7 3.5 %collective-permute-done.21 = bf16[592,384]{1,0:T(8,128)(2,1)S(1)} collective-permute-done((bf16[592,384]{1,0:T(8,128)(2,1)S(1)}, bf16[592,384]{1,0:T(8,128)(2,1)S(1)}, u32[]{:S(2)}, u32[]{:S(2)}) %collective-permute-start.21) | collective-permute-done | bytes 454688 | tf_op jit(solution)/shard_map/ppermute | solution.py:16
  165.6 7.5 %collective-permute-done.22 = bf16[592,384]{1,0:T(8,128)(2,1)S(1)} collective-permute-done((bf16[592,384]{1,0:T(8,128)(2,1)}, bf16[592,384]{1,0:T(8,128)(2,1)S(1)}, u32[]{:S(2)}, u32[]{:S(2)}) %collective-permute-start.22) | collective-permute-done | bytes 454688 | tf_op jit(solution)/shard_map/ppermute | solution.py:16
  176.0 2.6 pad_maximum_fusion.1
  181.1 2.2 copy.27
  183.3 2.4 pad_maximum_fusion.2.tokens_ref
  185.7 2.7 collective-permute-done.25.refs_5_
  188.4 23.7 %collective-permute-done.29.refs_9_ = bf16[1,768,768]{2,1,0:T(8,128)(2,1)} collective-permute-done((bf16[1,768,768]{2,1,0:T(8,128)(2,1)}, bf16[1,768,768]{2,1,0:T(8,128)(2,1)}, u32[]{:S(2)}, u32[]{:S(2)}) %collective-permute-start.29) | collective-permute-done | bytes 1179680 | tf_op jit(solution)/shard_map/ppermute | solution.py:16
  212.7 11.1 %layer_share.5 = (f32[1024,768]{1,0:T(8,128)}, bf16[1024,1536]{1,0:T(8,128)(2,1)}) custom-call(s32[2]{0:T(128)} %pad_add_fusion.2.place_ref, bf16[1024,592]{1,0:T(8,128)(2,1)} %pad_maximum_fusion.2.tokens_ref, f32[1024,1]{1,0:T(8,128)} %copy.28.scale_ref, f32[1,1536]{1,0:T(1,128)} %get-tuple-element.73.bias_ref, bf16[8,1536,768]{2,1,0:T(8,128)(2,1)} %tile_ref.13, ...), custom_call_target="tpu_custom_call" | custom-call | flops 4278190080 | bytes 13615104 | tf_op jit(solution)/shard_map/layer_share/pallas_call | solution.py:297
  223.8 10.8 %layer_share.6 = (f32[1024,768]{1,0:T(8,128)}, bf16[1024,1536]{1,0:T(8,128)(2,1)}) custom-call(s32[2]{0:T(128)} %pad_add_fusion.3.place_ref, bf16[1024,592]{1,0:T(8,128)(2,1)} %pad_maximum_fusion.2.tokens_ref, f32[1024,1]{1,0:T(8,128)} %copy.28.scale_ref, f32[1,1536]{1,0:T(1,128)} %get-tuple-element.72.bias_ref, ...), custom_call_target="tpu_custom_call", output_to_operand_aliasing={{0}: (6, {})} | custom-call | flops 4278190080 | bytes 13615104 | tf_op jit(solution)/shard_map/layer_share/pallas_call | solution.py:297
  234.6 10.7 %layer_share.7 = (f32[1024,768]{1,0:T(8,128)}, bf16[1024,1536]{1,0:T(8,128)(2,1)}) custom-call(s32[2]{0:T(128)} %pad_add_fusion.4.place_ref, bf16[1024,592]{1,0:T(8,128)(2,1)} %pad_maximum_fusion.2.tokens_ref, f32[1024,1]{1,0:T(8,128)} %copy.28.scale_ref, f32[1,1536]{1,0:T(1,128)} %get-tuple-element.71.bias_ref, ...), custom_call_target="tpu_custom_call", output_to_operand_aliasing={{0}: (9, {})} | custom-call | flops 4278190080 | bytes 13615104 | tf_op jit(solution)/shard_map/layer_share/pallas_call | solution.py:297
  246.6 7.5 %layer_share.8 = (bf16[512,768]{1,0:T(8,128)(2,1)}, bf16[512,1536]{1,0:T(8,128)(2,1)}) custom-call(s32[2]{0:T(128)} %pad_add_fusion.5.place_ref, bf16[1024,592]{1,0:T(8,128)(2,1)} %pad_maximum_fusion.2.tokens_ref, f32[1024,1]{1,0:T(8,128)} %copy.28.scale_ref, f32[1,1536]{1,0:T(1,128)} %get-tuple-element.70.bias_ref, bf16[8,1536,768]{2,1,0:T(8,128)(2,1)} %tile_ref.13, ...), custom_call_target="tpu_custom_call" | custom-call | flops 2139095040 | bytes 8896512 | tf_op jit(solution)/shard_map/layer_share/pallas_call | solution.py:297
  255.1 11.6 %came_sum.2 = (bf16[512,768]{1,0:T(8,128)(2,1)}, bf16[6144,1536]{1,0:T(8,128)(2,1)}) custom-call(s32[3]{0:T(128)} %pad_add_fusion.place_ref, bf16[1024,1536]{1,0:T(8,128)(2,1)} %get-tuple-element.42.refs_0_, bf16[1024,1536]{1,0:T(8,128)(2,1)} %get-tuple-element.44.refs_1_, ...), custom_call_target="tpu_custom_call", output_to_operand_aliasing={{1}: (13, {})} | custom-call | flops 4831838208 | bytes 15728640 | tf_op jit(solution)/shard_map/came_sum/pallas_call | solution.py:253
  270.5 7.8 %layer_share.9 = (f32[512,768]{1,0:T(8,128)}, bf16[512,1536]{1,0:T(8,128)(2,1)}) custom-call(s32[2]{0:T(128)} %pad_add_fusion.5.place_ref, bf16[1024,592]{1,0:T(8,128)(2,1)} %pad_maximum_fusion.2.tokens_ref, f32[1024,1]{1,0:T(8,128)} %copy.28.scale_ref, f32[1,1536]{1,0:T(1,128)} %get-tuple-element.70.bias_ref, bf16[8,1536,768]{2,1,0:T(8,128)(2,1)} %tile_ref.13, ...), custom_call_target="tpu_custom_call" | custom-call | flops 2139095040 | bytes 8896512 | tf_op jit(solution)/shard_map/layer_share/pallas_call | solution.py:297
  278.3 11.9 %came_sum.3 = f32[512,768]{1,0:T(8,128)} custom-call(s32[3]{0:T(128)} %pad_add_fusion.place_ref, bf16[1024,1536]{1,0:T(8,128)(2,1)} %get-tuple-element.42.refs_0_, bf16[1024,1536]{1,0:T(8,128)(2,1)} %get-tuple-element.44.refs_1_, bf16[1024,1536]{1,0:T(8,128)(2,1)} %get-tuple-element.46.refs_2_, bf16[512,1536]{1,0:T(8,128)(2,1)} %get-tuple-element.54.refs_3_, ...), custom_call_target="tpu_custom_call" | custom-call | flops 4831838208 | bytes 15728640 | tf_op jit(solution)/shard_map/came_sum/pallas_call | solution.py:253
  290.4 8.9 %collective-permute-done.6.refs_6_ = bf16[2,768,384]{2,1,0:T(8,128)(2,1)} collective-permute-done((bf16[2,768,384]{2,1,0:T(8,128)(2,1)}, bf16[2,768,384]{2,1,0:T(8,128)(2,1)}, u32[]{:S(2)}, u32[]{:S(2)}) %collective-permute-start.6) | collective-permute-done | bytes 1179680 | tf_op jit(solution)/shard_map/ppermute | solution.py:16
  300.0 3.9 %collective-permute-done.33 = bf16[512,768]{1,0:T(8,128)(2,1)} collective-permute-done((bf16[512,768]{1,0:T(8,128)(2,1)}, bf16[512,768]{1,0:T(8,128)(2,1)}, u32[]{:S(2)}, u32[]{:S(2)}) %collective-permute-start.33) | collective-permute-done | bytes 786464 | tf_op jit(solution)/shard_map/ppermute | solution.py:16
  305.9 1.8 fusion.14
  307.8 8.0 %collective-permute-done.34 = f32[528,128]{1,0:T(8,128)S(1)} collective-permute-done((f32[528,128]{1,0:T(8,128)S(1)}, f32[528,128]{1,0:T(8,128)S(1)}, u32[]{:S(2)}, u32[]{:S(2)}) %collective-permute-start.34) | collective-permute-done | bytes 270368 | tf_op jit(solution)/shard_map/ppermute | solution.py:16
  315.9 8.2 %shard_map.130 = bf16[1536,6144]{1,0:T(8,128)(2,1)} custom-call(s32[3]{0:T(128)} %pad_add_fusion.place_ref, bf16[2,768,384]{2,1,0:T(8,128)(2,1)} %collective-permute-done.refs_0_, bf16[2,768,384]{2,1,0:T(8,128)(2,1)} %collective-permute-done.1.refs_1_, bf16[2,768,384]{2,1,0:T(8,128)(2,1)} %collective-permute-done.2.refs_2_, ...), custom_call_target="tpu_custom_call", output_to_operand_aliasing={{}: (9, {})} | custom-call | flops 2831155200 | bytes 18874368 | tf_op jit(solution)/shard_map/pallas_call | solution.py:128
  324.1 5.5 %collective-permute-done.35 = f32[528,128]{1,0:T(8,128)S(1)} collective-permute-done((f32[528,128]{1,0:T(8,128)S(1)}, f32[528,128]{1,0:T(8,128)S(1)}, u32[]{:S(2)}, u32[]{:S(2)}) %collective-permute-start.35) | collective-permute-done | bytes 270368 | tf_op jit(solution)/shard_map/ppermute | solution.py:16
  (149 shorter events, 38.6 us)
Async XLA Ops:
  0.6 178.6 %copy-start = (f32[48,6144]{1,0:T(8,128)S(1)}, f32[48,6144]{1,0:T(8,128)}, u32[]{:S(2)}) copy-start(f32[48,6144]{1,0:T(8,128)} %param.20) | copy-start | bytes 3538948
  13.5 5.1 %collective-permute-start.8 = (f32[1613]{0:T(1024)S(1)}, f32[1613]{0:T(1024)S(1)}, u32[]{:S(2)}, u32[]{:S(2)}) collective-permute-start(f32[1613]{0:T(1024)S(1)} %concatenate.37), channel_id=1, source_target_pairs={{0,2},{2,0},{4,6},{6,4},{1,3},{3,1},{5,7},{7,5},{8,10},{10,8},{12,... | collective-permute-start | bytes 19364 | tf_op jit(solution)/shard_map/ppermute | solution.py:16
  16.5 29.2 %collective-permute-start.4 = (bf16[2,768,384]{2,1,0:T(8,128)(2,1)}, bf16[2,768,384]{2,1,0:T(8,128)(2,1)}, u32[]{:S(2)}, u32[]{:S(2)}) collective-permute-start(bf16[2,768,384]{2,1,0:T(8,128)(2,1)} %get-tuple-element.33), channel_id=1, source_target_pairs={{0,1},{1,0},{2,3},{3,2},{4,5},{5,4},{6,7},{7,6},{8,9},{9,8},{10,11... | collective-permute-start | bytes 3538952 | tf_op jit(solution)/shard_map/ppermute | solution.py:16
  18.0 51.5 %collective-permute-start = (bf16[2,768,384]{2,1,0:T(8,128)(2,1)}, bf16[2,768,384]{2,1,0:T(8,128)(2,1)}, u32[]{:S(2)}, u32[]{:S(2)}) collective-permute-start(bf16[2,768,384]{2,1,0:T(8,128)(2,1)} %get-tuple-element.32), channel_id=1, source_target_pairs={{0,1},{1,0},{2,3},{3,2},{4,5},{5,4},{6,7},{7,6},{8,9},{9,8},{10,11... | collective-permute-start | bytes 3538952 | tf_op jit(solution)/shard_map/ppermute | solution.py:16
  18.6 8.8 %collective-permute-start.9 = (f32[1613]{0:T(1024)S(1)}, f32[1613]{0:T(1024)S(1)}, u32[]{:S(2)}, u32[]{:S(2)}) collective-permute-start(f32[1613]{0:T(1024)S(1)} %add.157), channel_id=1, source_target_pairs={{0,4},{2,6},{4,0},{6,2},{1,5},{3,7},{5,1},{7,3},{8,12},{10,14},{12... | collective-permute-start | bytes 19364 | tf_op jit(solution)/shard_map/ppermute | solution.py:16
  29.6 48.9 %copy-start.11 = (bf16[592,1536]{1,0:T(8,128)(2,1)}, bf16[592,1536]{1,0:T(8,128)(2,1)S(1)}, u32[]{:S(2)}) copy-start(bf16[592,1536]{1,0:T(8,128)(2,1)S(1)} %maximum_maximum_fusion) | copy-start | bytes 5455876
  48.2 33.0 %collective-permute-start.13 = (bf16[592,384]{1,0:T(8,128)(2,1)}, bf16[592,384]{1,0:T(8,128)(2,1)}, u32[]{:S(2)}, u32[]{:S(2)}) collective-permute-start(bf16[592,384]{1,0:T(8,128)(2,1)} %fusion.12), channel_id=1, source_target_pairs={{0,4},{2,6},{4,0},{6,2},{1,5},{3,7},{5,1},{7,3},{8,12},{10,14},{12... | collective-permute-start | bytes 1363976 | tf_op jit(solution)/shard_map/ppermute | solution.py:16
  72.0 11.6 %collective-permute-start.14 = (bf16[592,384]{1,0:T(8,128)(2,1)}, bf16[592,384]{1,0:T(8,128)(2,1)}, u32[]{:S(2)}, u32[]{:S(2)}) collective-permute-start(bf16[592,384]{1,0:T(8,128)(2,1)} %fusion.13), channel_id=1, source_target_pairs={{0,2},{2,0},{4,6},{6,4},{1,3},{3,1},{5,7},{7,5},{8,10},{10,8},{12,... | collective-permute-start | bytes 1363976 | tf_op jit(solution)/shard_map/ppermute | solution.py:16
  74.9 20.4 %collective-permute-start.12 = (bf16[592,384]{1,0:T(8,128)(2,1)}, bf16[592,384]{1,0:T(8,128)(2,1)}, u32[]{:S(2)}, u32[]{:S(2)}) collective-permute-start(bf16[592,384]{1,0:T(8,128)(2,1)} %fusion.11), channel_id=1, source_target_pairs={{0,6},{2,4},{4,2},{6,0},{1,7},{3,5},{5,3},{7,1},{8,14},{10,12},{12... | collective-permute-start | bytes 1363976 | tf_op jit(solution)/shard_map/ppermute | solution.py:16
  98.0 37.2 %copy-start.8 = (bf16[592,384]{1,0:T(8,128)(2,1)}, bf16[592,384]{1,0:T(8,128)(2,1)S(1)}, u32[]{:S(2)}) copy-start(bf16[592,384]{1,0:T(8,128)(2,1)S(1)} %fusion.10) | copy-start | bytes 1363972
  98.0 21.2 %collective-permute-start.16 = (bf16[592,384]{1,0:T(8,128)(2,1)S(1)}, bf16[592,384]{1,0:T(8,128)(2,1)S(1)}, u32[]{:S(2)}, u32[]{:S(2)}) collective-permute-start(bf16[592,384]{1,0:T(8,128)(2,1)S(1)} %fusion.10), channel_id=1, source_target_pairs={{0,4},{2,6},{4,0},{6,2},{1,5},{3,7},{5,1},{7,3},{8,12},{10,14},{12... | collective-permute-start | bytes 1363976 | tf_op jit(solution)/shard_map/ppermute | solution.py:16
  105.0 37.9 %collective-permute-start.24 = (bf16[1,768,768]{2,1,0:T(8,128)(2,1)}, bf16[1,768,768]{2,1,0:T(8,128)(2,1)}, u32[]{:S(2)}, u32[]{:S(2)}) collective-permute-start(bf16[1,768,768]{2,1,0:T(8,128)(2,1)} %get-tuple-element.69), channel_id=1, source_target_pairs={{0,1},{1,0},{2,3},{3,2},{4,5},{5,4},{6,7},{7,6},{8,9},{9,8},{10,11... | collective-permute-start | bytes 3538952 | tf_op jit(solution)/shard_map/ppermute | solution.py:16
  106.5 20.8 %collective-permute-start.15 = (bf16[592,384]{1,0:T(8,128)(2,1)S(1)}, bf16[592,384]{1,0:T(8,128)(2,1)S(1)}, u32[]{:S(2)}, u32[]{:S(2)}) collective-permute-start(bf16[592,384]{1,0:T(8,128)(2,1)S(1)} %fusion.10), channel_id=1, source_target_pairs={{0,2},{2,0},{4,6},{6,4},{1,3},{3,1},{5,7},{7,5},{8,10},{10,8},{12,... | collective-permute-start | bytes 1363976 | tf_op jit(solution)/shard_map/ppermute | solution.py:16
  119.2 23.3 %copy-start.9 = (bf16[592,384]{1,0:T(8,128)(2,1)}, bf16[592,384]{1,0:T(8,128)(2,1)S(1)}, u32[]{:S(2)}) copy-start(bf16[592,384]{1,0:T(8,128)(2,1)S(1)} %collective-permute-done.16) | copy-start | bytes 1363972
  119.2 16.0 %collective-permute-start.17 = (bf16[592,384]{1,0:T(8,128)(2,1)S(1)}, bf16[592,384]{1,0:T(8,128)(2,1)}, u32[]{:S(2)}, u32[]{:S(2)}) collective-permute-start(bf16[592,384]{1,0:T(8,128)(2,1)S(1)} %collective-permute-done.16), channel_id=1, source_target_pairs={{0,2},{2,0},{4,6},{6,4},{1,3},{3,1},{5,7},{7,5},{8,10},{10,8},{12,... | collective-permute-start | bytes 1363976 | tf_op jit(solution)/shard_map/ppermute | solution.py:16
  120.7 17.2 %copy-start.4 = (bf16[512,588]{1,0:T(8,128)(2,1)}, bf16[512,588]{1,0:T(8,128)(2,1)S(1)}, u32[]{:S(2)}) copy-start(bf16[512,588]{1,0:T(8,128)(2,1)S(1)} %copy.25) | copy-start | bytes 1806340
  121.4 21.0 %collective-permute-start.19 = (bf16[592,384]{1,0:T(8,128)(2,1)S(1)}, bf16[592,384]{1,0:T(8,128)(2,1)}, u32[]{:S(2)}, u32[]{:S(2)}) collective-permute-start(bf16[592,384]{1,0:T(8,128)(2,1)S(1)} %fusion.10), channel_id=1, source_target_pairs={{0,16},{8,24},{16,0},{24,8},{1,17},{9,25},{17,1},{25,9},{2,18},{10... | collective-permute-start | bytes 1363976 | tf_op jit(solution)/shard_map/ppermute | solution.py:16
  122.9 18.0 %collective-permute-start.11 = (f32[512]{0:T(512)S(1)}, f32[512]{0:T(512)S(1)}, u32[]{:S(2)}, u32[]{:S(2)}) collective-permute-start(f32[512]{0:T(512)S(1)} %fusion.49), channel_id=1, source_target_pairs={{0,1},{1,0},{2,3},{3,2},{4,5},{5,4},{6,7},{7,6},{8,9},{9,8},{10,11... | collective-permute-start | bytes 6152 | tf_op jit(solution)/shard_map/ppermute | solution.py:16
  127.3 10.5 %copy-start.10 = (bf16[592,384]{1,0:T(8,128)(2,1)}, bf16[592,384]{1,0:T(8,128)(2,1)S(1)}, u32[]{:S(2)}) copy-start(bf16[592,384]{1,0:T(8,128)(2,1)S(1)} %collective-permute-done.15) | copy-start | bytes 1363972
  137.8 74.8 %collective-permute-start.18 = (bf16[4,592,384]{2,1,0:T(8,128)(2,1)}, bf16[4,592,384]{2,1,0:T(8,128)(2,1)}, u32[]{:S(2)}, u32[]{:S(2)}) collective-permute-start(bf16[4,592,384]{2,1,0:T(8,128)(2,1)} %pad_maximum_fusion), channel_id=1, source_target_pairs={{0,8},{8,0},{16,24},{24,16},{1,9},{9,1},{17,25},{25,17},{2,10},{10... | collective-permute-start | bytes 5455880 | tf_op jit(solution)/shard_map/ppermute | solution.py:16
  140.4 38.2 %collective-permute-start.10 = (bf16[512,592]{0,1:T(8,128)(2,1)}, bf16[512,592]{0,1:T(8,128)(2,1)}, u32[]{:S(2)}, u32[]{:S(2)}) collective-permute-start(bf16[512,592]{0,1:T(8,128)(2,1)} %copy.26), channel_id=1, source_target_pairs={{0,1},{1,0},{2,3},{3,2},{4,5},{5,4},{6,7},{7,6},{8,9},{9,8},{10,11... | collective-permute-start | bytes 1818632 | tf_op jit(solution)/shard_map/ppermute | solution.py:16
  140.9 18.2 %collective-permute-start.20 = (bf16[592,384]{1,0:T(8,128)(2,1)}, bf16[592,384]{1,0:T(8,128)(2,1)S(1)}, u32[]{:S(2)}, u32[]{:S(2)}) collective-permute-start(bf16[592,384]{1,0:T(8,128)(2,1)} %copy-done.10), channel_id=1, source_target_pairs={{0,16},{8,24},{16,0},{24,8},{1,17},{9,25},{17,1},{25,9},{2,18},{10... | collective-permute-start | bytes 1363976 | tf_op jit(solution)/shard_map/ppermute | solution.py:16
  142.4 21.7 %collective-permute-start.21 = (bf16[592,384]{1,0:T(8,128)(2,1)S(1)}, bf16[592,384]{1,0:T(8,128)(2,1)S(1)}, u32[]{:S(2)}, u32[]{:S(2)}) collective-permute-start(bf16[592,384]{1,0:T(8,128)(2,1)S(1)} %collective-permute-done.16), channel_id=1, source_target_pairs={{0,16},{8,24},{16,0},{24,8},{1,17},{9,25},{17,1},{25,9},{2,18},{10... | collective-permute-start | bytes 1363976 | tf_op jit(solution)/shard_map/ppermute | solution.py:16
  142.9 30.2 %collective-permute-start.22 = (bf16[592,384]{1,0:T(8,128)(2,1)}, bf16[592,384]{1,0:T(8,128)(2,1)S(1)}, u32[]{:S(2)}, u32[]{:S(2)}) collective-permute-start(bf16[592,384]{1,0:T(8,128)(2,1)} %collective-permute-done.17), channel_id=1, source_target_pairs={{0,16},{8,24},{16,0},{24,8},{1,17},{9,25},{17,1},{25,9},{2,18},{10... | collective-permute-start | bytes 1363976 | tf_op jit(solution)/shard_map/ppermute | solution.py:16
  159.1 19.4 %copy-start.12 = (bf16[592,384]{1,0:T(8,128)(2,1)}, bf16[592,384]{1,0:T(8,128)(2,1)S(1)}, u32[]{:S(2)}) copy-start(bf16[592,384]{1,0:T(8,128)(2,1)S(1)} %collective-permute-done.20) | copy-start | bytes 1363972
  159.1 29.2 %collective-permute-start.25 = (bf16[1,768,768]{2,1,0:T(8,128)(2,1)}, bf16[1,768,768]{2,1,0:T(8,128)(2,1)}, u32[]{:S(2)}, u32[]{:S(2)}) collective-permute-start(bf16[1,768,768]{2,1,0:T(8,128)(2,1)} %get-tuple-element.68), channel_id=1, source_target_pairs={{0,1},{1,0},{2,3},{3,2},{4,5},{5,4},{6,7},{7,6},{8,9},{9,8},{10,11... | collective-permute-start | bytes 3538952 | tf_op jit(solution)/shard_map/ppermute | solution.py:16
  164.2 14.4 %copy-start.13 = (bf16[592,384]{1,0:T(8,128)(2,1)}, bf16[592,384]{1,0:T(8,128)(2,1)S(1)}, u32[]{:S(2)}) copy-start(bf16[592,384]{1,0:T(8,128)(2,1)S(1)} %collective-permute-done.21) | copy-start | bytes 1363972
  164.2 47.9 %collective-permute-start.29 = (bf16[1,768,768]{2,1,0:T(8,128)(2,1)}, bf16[1,768,768]{2,1,0:T(8,128)(2,1)}, u32[]{:S(2)}, u32[]{:S(2)}) collective-permute-start(bf16[1,768,768]{2,1,0:T(8,128)(2,1)} %get-tuple-element.67), channel_id=1, source_target_pairs={{0,1},{1,0},{2,3},{3,2},{4,5},{5,4},{6,7},{7,6},{8,9},{9,8},{10,11... | collective-permute-start | bytes 3538952 | tf_op jit(solution)/shard_map/ppermute | solution.py:16
  173.2 5.4 %copy-start.14 = (bf16[592,384]{1,0:T(8,128)(2,1)}, bf16[592,384]{1,0:T(8,128)(2,1)S(1)}, u32[]{:S(2)}) copy-start(bf16[592,384]{1,0:T(8,128)(2,1)S(1)} %collective-permute-done.22) | copy-start | bytes 1363972
  173.2 38.9 %collective-permute-start.28 = (bf16[1,768,768]{2,1,0:T(8,128)(2,1)}, bf16[1,768,768]{2,1,0:T(8,128)(2,1)}, u32[]{:S(2)}, u32[]{:S(2)}) collective-permute-start(bf16[1,768,768]{2,1,0:T(8,128)(2,1)} %collective-permute-done.24.refs_4_), channel_id=1, source_target_pairs={{0,16},{8,24},{16,0},{24,8},{1,17},{9,25},{17,1},{25,9},{2,18},{10... | collective-permute-start | bytes 3538952 | tf_op jit(solution)/shard_map/ppermute | solution.py:16
  178.6 66.7 %collective-permute-start.23 = (bf16[4,592,384]{2,1,0:T(8,128)(2,1)}, bf16[4,592,384]{2,1,0:T(8,128)(2,1)S(1)}, u32[]{:S(2)}, u32[]{:S(2)}) collective-permute-start(bf16[4,592,384]{2,1,0:T(8,128)(2,1)} %pad_maximum_fusion.1), channel_id=1, source_target_pairs={{0,8},{8,0},{16,24},{24,16},{1,9},{9,1},{17,25},{25,17},{2,10},{10... | collective-permute-start | bytes 5455880 | tf_op jit(solution)/shard_map/ppermute | solution.py:16
  188.4 65.7 %collective-permute-start.26 = (bf16[1,768,768]{2,1,0:T(8,128)(2,1)}, bf16[1,768,768]{2,1,0:T(8,128)(2,1)S(1)}, u32[]{:S(2)}, u32[]{:S(2)}) collective-permute-start(bf16[1,768,768]{2,1,0:T(8,128)(2,1)} %collective-permute-done.24.refs_4_), channel_id=1, source_target_pairs={{0,8},{8,0},{16,24},{24,16},{1,9},{9,1},{17,25},{25,17},{2,10},{10... | collective-permute-start | bytes 3538952 | tf_op jit(solution)/shard_map/ppermute | solution.py:16
  212.1 42.9 %collective-permute-start.27 = (bf16[1,768,768]{2,1,0:T(8,128)(2,1)}, bf16[1,768,768]{2,1,0:T(8,128)(2,1)}, u32[]{:S(2)}, u32[]{:S(2)}) collective-permute-start(bf16[1,768,768]{2,1,0:T(8,128)(2,1)} %collective-permute-done.25.refs_5_), channel_id=1, source_target_pairs={{0,8},{8,0},{16,24},{24,16},{1,9},{9,1},{17,25},{25,17},{2,10},{10... | collective-permute-start | bytes 3538952 | tf_op jit(solution)/shard_map/ppermute | solution.py:16
  212.1 42.9 %collective-permute-start.31 = (bf16[1,768,768]{2,1,0:T(8,128)(2,1)}, bf16[1,768,768]{2,1,0:T(8,128)(2,1)}, u32[]{:S(2)}, u32[]{:S(2)}) collective-permute-start(bf16[1,768,768]{2,1,0:T(8,128)(2,1)} %collective-permute-done.29.refs_9_), channel_id=1, source_target_pairs={{0,8},{8,0},{16,24},{24,16},{1,9},{9,1},{17,25},{25,17},{2,10},{10... | collective-permute-start | bytes 3538952 | tf_op jit(solution)/shard_map/ppermute | solution.py:16
  212.6 42.4 %collective-permute-start.30 = (bf16[1,768,768]{2,1,0:T(8,128)(2,1)}, bf16[1,768,768]{2,1,0:T(8,128)(2,1)}, u32[]{:S(2)}, u32[]{:S(2)}) collective-permute-start(bf16[1,768,768]{2,1,0:T(8,128)(2,1)} %collective-permute-done.28.refs_8_), channel_id=1, source_target_pairs={{0,8},{8,0},{16,24},{24,16},{1,9},{9,1},{17,25},{25,17},{2,10},{10... | collective-permute-start | bytes 3538952 | tf_op jit(solution)/shard_map/ppermute | solution.py:16
  245.3 44.9 %collective-permute-start.2 = (bf16[2,768,384]{2,1,0:T(8,128)(2,1)}, bf16[2,768,384]{2,1,0:T(8,128)(2,1)}, u32[]{:S(2)}, u32[]{:S(2)}) collective-permute-start(bf16[2,768,384]{2,1,0:T(8,128)(2,1)} %collective-permute-done.refs_0_), channel_id=1, source_target_pairs={{0,16},{8,24},{16,0},{24,8},{1,17},{9,25},{17,1},{25,9},{2,18},{10... | collective-permute-start | bytes 3538952 | tf_op jit(solution)/shard_map/ppermute | solution.py:16
  254.0 45.3 %collective-permute-start.6 = (bf16[2,768,384]{2,1,0:T(8,128)(2,1)}, bf16[2,768,384]{2,1,0:T(8,128)(2,1)}, u32[]{:S(2)}, u32[]{:S(2)}) collective-permute-start(bf16[2,768,384]{2,1,0:T(8,128)(2,1)} %collective-permute-done.4.refs_4_), channel_id=1, source_target_pairs={{0,16},{8,24},{16,0},{24,8},{1,17},{9,25},{17,1},{25,9},{2,18},{10... | collective-permute-start | bytes 3538952 | tf_op jit(solution)/shard_map/ppermute | solution.py:16
  255.1 13.2 %copy-start.15 = (bf16[1536,128]{1,0:T(8,128)(2,1)S(1)}, bf16[1536,128]{1,0:T(8,128)(2,1)}, u32[]{:S(2)}) copy-start(bf16[1536,128]{1,0:T(8,128)(2,1)} %param.23) | copy-start | bytes 1179652
  266.7 32.6 %collective-permute-start.32 = (bf16[512,768]{1,0:T(8,128)(2,1)}, bf16[512,768]{1,0:T(8,128)(2,1)S(1)}, u32[]{:S(2)}, u32[]{:S(2)}) collective-permute-start(bf16[512,768]{1,0:T(8,128)(2,1)} %get-tuple-element.53), channel_id=1, source_target_pairs={{0,1},{1,0},{2,3},{3,2},{4,5},{5,4},{6,7},{7,6},{8,9},{9,8},{10,11... | collective-permute-start | bytes 2359304 | tf_op jit(solution)/shard_map/ppermute | solution.py:16
  269.7 46.1 %collective-permute-start.1 = (bf16[2,768,384]{2,1,0:T(8,128)(2,1)}, bf16[2,768,384]{2,1,0:T(8,128)(2,1)}, u32[]{:S(2)}, u32[]{:S(2)}) collective-permute-start(bf16[2,768,384]{2,1,0:T(8,128)(2,1)} %collective-permute-done.refs_0_), channel_id=1, source_target_pairs={{0,8},{8,0},{16,24},{24,16},{1,9},{9,1},{17,25},{25,17},{2,10},{10... | collective-permute-start | bytes 3538952 | tf_op jit(solution)/shard_map/ppermute | solution.py:16
  270.0 33.9 %collective-permute-start.33 = (bf16[512,768]{1,0:T(8,128)(2,1)}, bf16[512,768]{1,0:T(8,128)(2,1)}, u32[]{:S(2)}, u32[]{:S(2)}) collective-permute-start(bf16[512,768]{1,0:T(8,128)(2,1)} %get-tuple-element.55), channel_id=1, source_target_pairs={{0,1},{1,0},{2,3},{3,2},{4,5},{5,4},{6,7},{7,6},{8,9},{9,8},{10,11... | collective-permute-start | bytes 2359304 | tf_op jit(solution)/shard_map/ppermute | solution.py:16
  278.3 21.5 %copy-start.16 = (f32[512,768]{1,0:T(8,128)S(1)}, f32[512,768]{1,0:T(8,128)}, u32[]{:S(2)}) copy-start(f32[512,768]{1,0:T(8,128)} %get-tuple-element.52) | copy-start | bytes 4718596
  290.2 25.6 %collective-permute-start.5 = (bf16[2,768,384]{2,1,0:T(8,128)(2,1)}, bf16[2,768,384]{2,1,0:T(8,128)(2,1)}, u32[]{:S(2)}, u32[]{:S(2)}) collective-permute-start(bf16[2,768,384]{2,1,0:T(8,128)(2,1)} %collective-permute-done.4.refs_4_), channel_id=1, source_target_pairs={{0,8},{8,0},{16,24},{24,16},{1,9},{9,1},{17,25},{25,17},{2,10},{10... | collective-permute-start | bytes 3538952 | tf_op jit(solution)/shard_map/ppermute | solution.py:16
  299.3 16.6 %collective-permute-start.3 = (bf16[2,768,384]{2,1,0:T(8,128)(2,1)}, bf16[2,768,384]{2,1,0:T(8,128)(2,1)}, u32[]{:S(2)}, u32[]{:S(2)}) collective-permute-start(bf16[2,768,384]{2,1,0:T(8,128)(2,1)} %collective-permute-done.2.refs_2_), channel_id=1, source_target_pairs={{0,8},{8,0},{16,24},{24,16},{1,9},{9,1},{17,25},{25,17},{2,10},{10... | collective-permute-start | bytes 3538952 | tf_op jit(solution)/shard_map/ppermute | solution.py:16
  299.3 16.6 %collective-permute-start.7 = (bf16[2,768,384]{2,1,0:T(8,128)(2,1)}, bf16[2,768,384]{2,1,0:T(8,128)(2,1)}, u32[]{:S(2)}, u32[]{:S(2)}) collective-permute-start(bf16[2,768,384]{2,1,0:T(8,128)(2,1)} %collective-permute-done.6.refs_6_), channel_id=1, source_target_pairs={{0,8},{8,0},{16,24},{24,16},{1,9},{9,1},{17,25},{25,17},{2,10},{10... | collective-permute-start | bytes 3538952 | tf_op jit(solution)/shard_map/ppermute | solution.py:16
  307.7 8.0 %collective-permute-start.34 = (f32[528,128]{1,0:T(8,128)S(1)}, f32[528,128]{1,0:T(8,128)S(1)}, u32[]{:S(2)}, u32[]{:S(2)}) collective-permute-start(f32[528,128]{1,0:T(8,128)S(1)} %pad_maximum_fusion.4), channel_id=1, source_target_pairs={{0,2},{2,0},{4,6},{6,4},{1,3},{3,1},{5,7},{7,5},{8,10},{10,8},{12,... | collective-permute-start | bytes 811016 | tf_op jit(solution)/shard_map/ppermute | solution.py:16
  315.8 13.9 %collective-permute-start.35 = (f32[528,128]{1,0:T(8,128)S(1)}, f32[528,128]{1,0:T(8,128)S(1)}, u32[]{:S(2)}, u32[]{:S(2)}) collective-permute-start(f32[528,128]{1,0:T(8,128)S(1)} %fusion.50), channel_id=1, source_target_pairs={{0,4},{2,6},{4,0},{6,2},{1,5},{3,7},{5,1},{7,3},{8,12},{10,14},{12... | collective-permute-start | bytes 811016 | tf_op jit(solution)/shard_map/ppermute | solution.py:16
  315.9 14.7 %copy-start.1 = (f32[48,6144]{1,0:T(8,128)S(1)}, f32[48,6144]{1,0:T(8,128)}, u32[]{:S(2)}) copy-start(f32[48,6144]{1,0:T(8,128)} %param.20) | copy-start | bytes 3538948
  (14 other events, 40.3 us)
